TPU v7x, 32 devices: a whole 2x2x4 slice. The times are simulated.
32 devices in a mesh: ta: 2 (over x), ha: 4 (over y, core), wa: 4 (over z).
Axes of the slice: x: 2, y: 2, z: 4, core: 2. Of those that a mesh axis runs over, the one named last changes fastest.
Arguments:
- volume: bfloat16 [2, 128, 64, 128], P('ta', 'ha', 'wa'), may hold values from -6 to 6
- cotangent: bfloat16 [2, 128, 64, 128], P('ta', 'ha', 'wa'), may hold values from -6 to 6
- kernel_one: bfloat16 [3, 3, 3, 128, 128], replicated, may hold values from -0.109375 to 0.109375
- kernel_two: bfloat16 [3, 3, 3, 128, 128], replicated, may hold values from -0.109375 to 0.109375
Outputs:
- d_volume: bfloat16 [2, 128, 64, 128], P('ta', 'ha', 'wa')
- grad_one: float32 [3, 3, 3, 128, 128], replicated
- grad_two: float32 [3, 3, 3, 128, 128], replicated
All inputs are finite; a program needn't handle non-finite values.
Results may differ from a plain program's by a relative error of at most 0.0049.
Values may be sent and summed in bfloat16 or wider, within the bound.
A program may use at most 64 MiB of HBM per device.

v0:
```python
import jax
import jax.numpy as jnp
from jax import lax
from jax.sharding import PartitionSpec as P


def padded_2(cells, sides, width):
    for axis, dim in sides:
        count = lax.axis_size(axis)
        ends = count - 1
        head = lax.slice_in_dim(cells, 0, width, axis=dim)
        tail = lax.slice_in_dim(cells, cells.shape[dim] - width, cells.shape[dim], axis=dim)
        cells = jnp.concatenate(
            [
                lax.ppermute(tail, axis, [(i, (i + 1) % count) for i in range(ends)]),
                cells,
                lax.ppermute(head, axis, [((i + 1) % count, i) for i in range(ends)]),
            ],
            axis=dim,
        )
    return cells


def flip_swap(kernel):
    return jnp.swapaxes(kernel[::-1, ::-1, ::-1], 3, 4)


def window_rows(padded, offset_t, offset_h):
    frames = padded.shape[0] - 2
    height = padded.shape[1] - 2
    width = padded.shape[2] - 2
    chans = padded.shape[3]
    pieces = [
        padded[offset_t : offset_t + frames, offset_h : offset_h + height, shift : shift + width]
        for shift in range(3)
    ]
    return jnp.concatenate(pieces, axis=-1).reshape(-1, 3 * chans)


def conv_local(padded, kernel):
    frames = padded.shape[0] - 2
    height = padded.shape[1] - 2
    width = padded.shape[2] - 2
    chans = padded.shape[3]
    total = jnp.zeros((frames * height * width, chans), jnp.float32)
    for offset_t in range(3):
        for offset_h in range(3):
            rows = window_rows(padded, offset_t, offset_h)
            total = total + jnp.dot(
                rows,
                kernel[offset_t, offset_h].reshape(3 * chans, chans),
                preferred_element_type=jnp.float32,
            )
    return total.reshape(frames, height, width, chans)


def kernel_local(padded, other):
    chans = padded.shape[3]
    right = other.reshape(-1, chans)
    blocks = []
    for offset_t in range(3):
        for offset_h in range(3):
            rows = window_rows(padded, offset_t, offset_h)
            product = lax.dot_general(
                rows, right, (((0,), (0,)), ((), ())), preferred_element_type=jnp.float32
            )
            blocks.append(product.reshape(3, chans, chans))
    return jnp.stack(blocks).reshape(3, 3, 3, chans, chans)


def body(volume, cotangent, kernel_one, kernel_two):
    stacked = jnp.stack((volume, cotangent))
    padded_both = padded_2(stacked, (("ta", 1), ("ha", 2), ("wa", 3)), 1)
    volume_pad = padded_both[0]
    cotangent_pad = padded_both[1]
    pre = conv_local(volume_pad, kernel_one)
    sig = jax.nn.sigmoid(pre)
    hidden = (pre * sig).astype(jnp.bfloat16)
    d_hidden = conv_local(cotangent_pad, flip_swap(kernel_two))
    d_pre = (d_hidden * sig * (1.0 + pre * (1.0 - sig))).astype(jnp.bfloat16)
    total_cells = (
        volume.shape[0]
        * volume.shape[1]
        * volume.shape[2]
        * lax.axis_size("ta")
        * lax.axis_size("ha")
        * lax.axis_size("wa")
    )
    scale = 1.0 / jnp.sqrt(jnp.float32(total_cells))
    part_two = flip_swap(kernel_local(cotangent_pad, hidden))
    d_pre_pad = padded_2(d_pre, (("ta", 0), ("ha", 1), ("wa", 2)), 1)
    d_volume = conv_local(d_pre_pad, flip_swap(kernel_one)).astype(jnp.bfloat16)
    part_one = kernel_local(volume_pad, d_pre)
    summed_one, summed_two = lax.psum((part_one, part_two), ("ta", "ha", "wa"))
    return (d_volume, summed_one * scale, summed_two * scale)


def solution(mesh):
    in_specs = (P("ta", "ha", "wa", None), P("ta", "ha", "wa", None), P(), P())
    out_specs = (P("ta", "ha", "wa", None), P(), P())
    return jax.shard_map(body, mesh=mesh, in_specs=in_specs, out_specs=out_specs, check_vma=False)
```

profile of v0, /device:TPU:0, one launch (start us, length us, event | category | flops | bytes accessed | tf_op | source)
XLA Modules:
  0.0 267.9 jit_solution(2284530957362747700)
XLA Ops:
  7.2 1.8 pad_maximum_fusion.40
  9.0 4.9 %collective-permute-start = (bf16[2,1,32,16,128]{4,3,2,1,0:T(8,128)(2,1)}, bf16[2,1,32,16,128]{4,3,2,1,0:T(8,128)(2,1)S(1)}, u32[]{:S(2)}, u32[]{:S(2)}) collective-permute-start(bf16[2,1,32,16,128]{4,3,2,1,0:T(8,128)(2,1)} %pad_maximum_fusion.40), channel_id=1, source_target_pairs={{0,16},{1,17},{2,18},{3,19},{4,20},{5,21},{6,22},{7,23},{8,24},{9,... | collective-permute-start | bytes 786440 | tf_op jit(solution)/shard_map/ppermute | solution.py:15
  13.9 1.3 collective-permute-start.1
  15.2 2.2 fusion.57
  17.4 1.4 copy.26
  18.9 1.4 copy.27
  20.3 1.0 fusion.56
  21.3 2.4 collective-permute-done.1
  23.8 1.3 collective-permute-start.2
  25.1 1.3 collective-permute-start.3
  26.5 3.4 %collective-permute-done.3 = bf16[2,3,1,16,128]{4,3,2,1,0:T(8,128)(2,1)S(1)} collective-permute-done((bf16[2,3,1,16,128]{4,3,2,1,0:T(8,128)(2,1)S(1)}, bf16[2,3,1,16,128]{4,3,2,1,0:T(8,128)(2,1)S(1)}, u32[]{:S(2)}, u32[]{:S(2)}) %collective-permute-start.3) | collective-permute-done | bytes 24608 | tf_op jit(solution)/shard_map/ppermute | solution.py:17
  30.1 3.5 %collective-permute-start.4 = (bf16[2,3,34,1,128]{4,3,2,1,0:T(2,128)(2,1)S(1)}, bf16[2,3,34,1,128]{4,3,2,1,0:T(2,128)(2,1)S(1)}, u32[]{:S(2)}, u32[]{:S(2)}) collective-permute-start(bf16[2,3,34,1,128]{4,3,2,1,0:T(2,128)(2,1)S(1)} %get-tuple-element.34), channel_id=1, source_target_pairs={{0,1},{1,2},{2,3},{4,5},{5,6},{6,7},{8,9},{9,10},{10,11},{12,13},{... | collective-permute-start | bytes 156680 | tf_op jit(solution)/shard_map/ppermute | solution.py:15
  33.6 1.3 collective-permute-start.5
  35.8 4.3 %collective-permute-done.5 = bf16[2,3,34,1,128]{4,3,2,1,0:T(2,128)(2,1)S(1)} collective-permute-done((bf16[2,3,34,1,128]{4,3,2,1,0:T(2,128)(2,1)S(1)}, bf16[2,3,34,1,128]{4,3,2,1,0:T(2,128)(2,1)S(1)}, u32[]{:S(2)}, u32[]{:S(2)}) %collective-permute-start.5) | collective-permute-done | bytes 52256 | tf_op jit(solution)/shard_map/ppermute | solution.py:17
  41.2 1.5 fusion.62
  42.6 1.1 fusion.61
  43.8 1.1 fusion.60
  45.9 1.9 fusion.65
  47.8 1.0 copy.37
  48.8 1.9 fusion.64
  56.7 1.1 pad_maximum_fusion.27
  59.7 1.1 pad_maximum_fusion.30
  61.7 1.1 pad_maximum_fusion.31
  63.8 2.2 pad_maximum_fusion.32
  66.0 1.9 copy.31
  67.9 1.9 copy.32
  69.8 2.2 pad_maximum_fusion.34
  72.0 1.9 copy.33
  73.9 1.9 copy.34
  75.8 2.2 pad_maximum_fusion.36
  78.0 1.9 copy.35
  79.9 2.0 copy.36
  81.9 1.3 convolution_add_fusion.15
  83.2 1.2 convolution_add_fusion.14
  89.1 2.3 collective-permute-start.6
  91.5 1.5 collective-permute-start.7
  97.9 1.7 collective-permute-done.7
  99.6 1.9 collective-permute-start.8
  101.5 1.3 collective-permute-start.9
  103.1 1.2 copy-done.9
  104.3 2.4 copy.46
  106.8 3.5 %collective-permute-start.10 = (bf16[3,34,1,128]{3,2,1,0:T(2,128)(2,1)S(1)}, bf16[3,34,1,128]{3,2,1,0:T(2,128)(2,1)S(1)}, u32[]{:S(2)}, u32[]{:S(2)}) collective-permute-start(bf16[3,34,1,128]{3,2,1,0:T(2,128)(2,1)S(1)} %get-tuple-element.112), channel_id=1, source_target_pairs={{0,1},{1,2},{2,3},{4,5},{5,6},{6,7},{8,9},{9,10},{10,11},{12,13},{... | collective-permute-start | bytes 78344 | tf_op jit(solution)/shard_map/ppermute | solution.py:15
  110.3 1.3 collective-permute-start.11
  111.6 1.4 reverse_bitcast_fusion
  113.0 3.3 %collective-permute-done.11 = bf16[3,34,1,128]{3,2,1,0:T(2,128)(2,1)S(1)} collective-permute-done((bf16[3,34,1,128]{3,2,1,0:T(2,128)(2,1)S(1)}, bf16[3,34,1,128]{3,2,1,0:T(2,128)(2,1)S(1)}, u32[]{:S(2)}, u32[]{:S(2)}) %collective-permute-start.11) | collective-permute-done | bytes 26144 | tf_op jit(solution)/shard_map/ppermute | solution.py:17
  122.2 134.4 %all-reduce.3.cloned.1.call-done = (f32[3,3,3,128,128]{4,3,2,1,0:T(8,128)}, f32[3,3,3,128,128]{4,3,2,1,0:T(8,128)}) async-done(((f32[3,3,3,128,128]{4,3,2,1,0:T(8,128)}, f32[3,3,3,128,128]{4,3,2,1,0:T(8,128)}), (f32[3,3,3,128,128]{4,3,2,1,0:T(8,128)}, f32[3,3,3,128,128]{4,3,2,1,0:T(8,128)})) %all-reduce.3.cloned.1.call-update) | async-done | bytes 3538960 | tf_op jit(solution)/shard_map/psum | solution.py:94
  256.7 3.0 %broadcast_multiply_fusion = f32[3,3,3,128,128]{4,3,2,1,0:T(8,128)} fusion(f32[3,3,3,128,128]{4,3,2,1,0:T(8,128)} %get-tuple-element.4), kind=kLoop, calls=%fused_computation.63 | loop fusion | flops 442368 | bytes 3538944 | tf_op jit(solution)/shard_map/mul | solution.py:95
  259.7 1.4 broadcast_multiply_fusion.1
  (211 shorter events, 28.1 us)
Async XLA Ops:
  7.2 10.2 %copy-start.33 = (bf16[3,3,3,128,128]{4,3,2,1,0:T(8,128)(2,1)S(1)}, bf16[3,3,3,128,128]{4,3,2,1,0:T(8,128)(2,1)}, u32[]{:S(2)}) copy-start(bf16[3,3,3,128,128]{4,3,2,1,0:T(8,128)(2,1)} %param.7) | copy-start | bytes 2654212
  7.2 249.5 %all-reduce.3.cloned.1.call-start = ((), (), s32[]{:S(2)}) async-start(), calls=%async_computation | async-start | bytes 7077888 | tf_op jit(solution)/shard_map/psum | solution.py:94
  9.0 12.3 %collective-permute-start = (bf16[2,1,32,16,128]{4,3,2,1,0:T(8,128)(2,1)}, bf16[2,1,32,16,128]{4,3,2,1,0:T(8,128)(2,1)S(1)}, u32[]{:S(2)}, u32[]{:S(2)}) collective-permute-start(bf16[2,1,32,16,128]{4,3,2,1,0:T(8,128)(2,1)} %pad_maximum_fusion.40), channel_id=1, source_target_pairs={{0,16},{1,17},{2,18},{3,19},{4,20},{5,21},{6,22},{7,23},{8,24},{9,... | collective-permute-start | bytes 786440 | tf_op jit(solution)/shard_map/ppermute | solution.py:15
  13.9 9.9 %collective-permute-start.1 = (bf16[2,1,32,16,128]{4,3,2,1,0:T(8,128)(2,1)}, bf16[2,1,32,16,128]{4,3,2,1,0:T(8,128)(2,1)S(1)}, u32[]{:S(2)}, u32[]{:S(2)}) collective-permute-start(bf16[2,1,32,16,128]{4,3,2,1,0:T(8,128)(2,1)} %pad_maximum_fusion.40), channel_id=1, source_target_pairs={{16,0},{17,1},{18,2},{19,3},{20,4},{21,5},{22,6},{23,7},{24,8},{25... | collective-permute-start | bytes 786440 | tf_op jit(solution)/shard_map/ppermute | solution.py:17
  17.4 1.5 copy-start
  18.9 4.8 %copy-start.10 = (bf16[1,32,16,128]{3,2,1,0:T(8,128)(2,1)S(1)}, bf16[1,32,16,128]{3,2,1,0:T(8,128)(2,1)}, u32[]{:S(2)}) copy-start(bf16[1,32,16,128]{3,2,1,0:T(8,128)(2,1)} %param.5) | copy-start | bytes 393220
  18.9 4.8 %copy-start.11 = (bf16[1,32,16,128]{3,2,1,0:T(8,128)(2,1)S(1)}, bf16[1,32,16,128]{3,2,1,0:T(8,128)(2,1)}, u32[]{:S(2)}) copy-start(bf16[1,32,16,128]{3,2,1,0:T(8,128)(2,1)} %param.4) | copy-start | bytes 393220
  23.8 2.7 %collective-permute-start.2 = (bf16[2,3,1,16,128]{4,3,2,1,0:T(8,128)(2,1)S(1)}, bf16[2,3,1,16,128]{4,3,2,1,0:T(8,128)(2,1)S(1)}, u32[]{:S(2)}, u32[]{:S(2)}) collective-permute-start(bf16[2,3,1,16,128]{4,3,2,1,0:T(8,128)(2,1)S(1)} %get-tuple-element.36), channel_id=1, source_target_pairs={{0,4},{4,8},{8,12},{1,5},{5,9},{9,13},{2,6},{6,10},{10,14},{3,7},{... | collective-permute-start | bytes 73736 | tf_op jit(solution)/shard_map/ppermute | solution.py:15
  25.1 4.8 %collective-permute-start.3 = (bf16[2,3,1,16,128]{4,3,2,1,0:T(8,128)(2,1)S(1)}, bf16[2,3,1,16,128]{4,3,2,1,0:T(8,128)(2,1)S(1)}, u32[]{:S(2)}, u32[]{:S(2)}) collective-permute-start(bf16[2,3,1,16,128]{4,3,2,1,0:T(8,128)(2,1)S(1)} %get-tuple-element.37), channel_id=1, source_target_pairs={{4,0},{8,4},{12,8},{5,1},{9,5},{13,9},{6,2},{10,6},{14,10},{7,3},{... | collective-permute-start | bytes 73736 | tf_op jit(solution)/shard_map/ppermute | solution.py:17
  30.1 5.7 %collective-permute-start.4 = (bf16[2,3,34,1,128]{4,3,2,1,0:T(2,128)(2,1)S(1)}, bf16[2,3,34,1,128]{4,3,2,1,0:T(2,128)(2,1)S(1)}, u32[]{:S(2)}, u32[]{:S(2)}) collective-permute-start(bf16[2,3,34,1,128]{4,3,2,1,0:T(2,128)(2,1)S(1)} %get-tuple-element.34), channel_id=1, source_target_pairs={{0,1},{1,2},{2,3},{4,5},{5,6},{6,7},{8,9},{9,10},{10,11},{12,13},{... | collective-permute-start | bytes 156680 | tf_op jit(solution)/shard_map/ppermute | solution.py:15
  33.6 6.6 %collective-permute-start.5 = (bf16[2,3,34,1,128]{4,3,2,1,0:T(2,128)(2,1)S(1)}, bf16[2,3,34,1,128]{4,3,2,1,0:T(2,128)(2,1)S(1)}, u32[]{:S(2)}, u32[]{:S(2)}) collective-permute-start(bf16[2,3,34,1,128]{4,3,2,1,0:T(2,128)(2,1)S(1)} %get-tuple-element.35), channel_id=1, source_target_pairs={{1,0},{2,1},{3,2},{5,4},{6,5},{7,6},{9,8},{10,9},{11,10},{13,12},{... | collective-permute-start | bytes 156680 | tf_op jit(solution)/shard_map/ppermute | solution.py:17
  44.8 2.9 %copy-start.37 = (bf16[1,32,16,128]{3,2,1,0:T(8,128)(2,1)S(1)}, bf16[1,32,16,128]{3,2,1,0:T(8,128)(2,1)}, u32[]{:S(2)}) copy-start(bf16[1,32,16,128]{3,2,1,0:T(8,128)(2,1)} %get-tuple-element.80) | copy-start | bytes 393220
  44.8 2.9 %copy-start.38 = (bf16[1,32,16,128]{3,2,1,0:T(8,128)(2,1)S(1)}, bf16[1,32,16,128]{3,2,1,0:T(8,128)(2,1)}, u32[]{:S(2)}) copy-start(bf16[1,32,16,128]{3,2,1,0:T(8,128)(2,1)} %get-tuple-element.81) | copy-start | bytes 393220
  44.8 2.9 %copy-start.39 = (bf16[1,32,16,128]{3,2,1,0:T(8,128)(2,1)S(1)}, bf16[1,32,16,128]{3,2,1,0:T(8,128)(2,1)}, u32[]{:S(2)}) copy-start(bf16[1,32,16,128]{3,2,1,0:T(8,128)(2,1)} %get-tuple-element.82) | copy-start | bytes 393220
  44.9 5.8 %copy-start.34 = (bf16[1,32,16,128]{3,2,1,0:T(8,128)(2,1)S(1)}, bf16[1,32,16,128]{3,2,1,0:T(8,128)(2,1)}, u32[]{:S(2)}) copy-start(bf16[1,32,16,128]{3,2,1,0:T(8,128)(2,1)} %get-tuple-element.77) | copy-start | bytes 393220
  44.9 5.8 %copy-start.35 = (bf16[1,32,16,128]{3,2,1,0:T(8,128)(2,1)S(1)}, bf16[1,32,16,128]{3,2,1,0:T(8,128)(2,1)}, u32[]{:S(2)}) copy-start(bf16[1,32,16,128]{3,2,1,0:T(8,128)(2,1)} %get-tuple-element.78) | copy-start | bytes 393220
  44.9 5.7 %copy-start.36 = (bf16[1,32,16,128]{3,2,1,0:T(8,128)(2,1)S(1)}, bf16[1,32,16,128]{3,2,1,0:T(8,128)(2,1)}, u32[]{:S(2)}) copy-start(bf16[1,32,16,128]{3,2,1,0:T(8,128)(2,1)} %get-tuple-element.79) | copy-start | bytes 393220
  47.8 3.9 %copy-start.40 = (bf16[1,32,16,128]{3,2,1,0:T(8,128)(2,1)S(1)}, bf16[1,32,16,128]{3,2,1,0:T(8,128)(2,1)}, u32[]{:S(2)}) copy-start(bf16[1,32,16,128]{3,2,1,0:T(8,128)(2,1)} %get-tuple-element.74) | copy-start | bytes 393220
  57.8 1.9 copy-start.1
  81.9 2.6 copy-start.4
  81.9 2.6 copy-start.61
  81.9 2.9 %copy-start.3 = (bf16[1,32,16,384]{3,2,1,0:T(8,128)(2,1)S(1)}, bf16[1,32,16,384]{3,2,1,0:T(8,128)(2,1)}, u32[]{:S(2)}) copy-start(bf16[1,32,16,384]{3,2,1,0:T(8,128)(2,1)} %get-tuple-element.140) | copy-start | bytes 1179652
  81.9 2.9 %copy-start.60 = (bf16[1,1,3,128,128]{4,3,2,1,0:T(8,128)(2,1)S(1)}, bf16[1,1,3,128,128]{4,3,2,1,0:T(8,128)(2,1)}, u32[]{:S(2)}) copy-start(bf16[1,1,3,128,128]{4,3,2,1,0:T(8,128)(2,1)} %get-tuple-element.29) | copy-start | bytes 294916
  83.2 1.9 copy-start.6
  83.2 1.9 copy-start.59
  88.3 4.6 %copy-start.14 = (bf16[512,384]{0,1:T(8,128)(2,1)S(1)}, bf16[512,384]{0,1:T(8,128)(2,1)}, u32[]{:S(2)}) copy-start(bf16[512,384]{0,1:T(8,128)(2,1)} %copy.37) | copy-start | bytes 1179652
  88.6 4.6 %copy-start.15 = (bf16[512,384]{0,1:T(8,128)(2,1)S(1)}, bf16[512,384]{0,1:T(8,128)(2,1)}, u32[]{:S(2)}) copy-start(bf16[512,384]{0,1:T(8,128)(2,1)} %copy.38) | copy-start | bytes 1179652
  88.6 4.9 %copy-start.16 = (bf16[512,384]{0,1:T(8,128)(2,1)S(1)}, bf16[512,384]{0,1:T(8,128)(2,1)}, u32[]{:S(2)}) copy-start(bf16[512,384]{0,1:T(8,128)(2,1)} %copy.39) | copy-start | bytes 1179652
  89.0 4.8 %copy-start.18 = (bf16[512,384]{0,1:T(8,128)(2,1)S(1)}, bf16[512,384]{0,1:T(8,128)(2,1)}, u32[]{:S(2)}) copy-start(bf16[512,384]{0,1:T(8,128)(2,1)} %copy.40) | copy-start | bytes 1179652
  89.0 5.1 %copy-start.17 = (bf16[512,384]{0,1:T(8,128)(2,1)S(1)}, bf16[512,384]{0,1:T(8,128)(2,1)}, u32[]{:S(2)}) copy-start(bf16[512,384]{0,1:T(8,128)(2,1)} %copy.41) | copy-start | bytes 1179652
  89.1 8.7 %collective-permute-start.6 = (bf16[1,32,16,128]{3,2,1,0:T(8,128)(2,1)S(1)}, bf16[1,32,16,128]{3,2,1,0:T(8,128)(2,1)S(1)}, u32[]{:S(2)}, u32[]{:S(2)}) collective-permute-start(bf16[1,32,16,128]{3,2,1,0:T(8,128)(2,1)S(1)} %multiply_convert_fusion.2), channel_id=1, source_target_pairs={{0,16},{1,17},{2,18},{3,19},{4,20},{5,21},{6,22},{7,23},{8,24},{9,... | collective-permute-start | bytes 393224 | tf_op jit(solution)/shard_map/ppermute | solution.py:15
  91.5 8.1 %collective-permute-start.7 = (bf16[1,32,16,128]{3,2,1,0:T(8,128)(2,1)S(1)}, bf16[1,32,16,128]{3,2,1,0:T(8,128)(2,1)S(1)}, u32[]{:S(2)}, u32[]{:S(2)}) collective-permute-start(bf16[1,32,16,128]{3,2,1,0:T(8,128)(2,1)S(1)} %multiply_convert_fusion.2), channel_id=1, source_target_pairs={{16,0},{17,1},{18,2},{19,3},{20,4},{21,5},{22,6},{23,7},{24,8},{25... | collective-permute-start | bytes 393224 | tf_op jit(solution)/shard_map/ppermute | solution.py:17
  92.9 1.4 copy-start.20
  94.1 1.4 copy-start.13
  94.4 1.4 copy-start.21
  94.7 1.4 copy-start.24
  95.0 1.4 copy-start.27
  95.2 1.4 copy-start.26
  95.5 1.4 copy-start.8
  95.8 1.5 copy-start.28
  96.1 1.5 copy-start.30
  96.7 6.1 %copy-start.25 = (bf16[512,384]{0,1:T(8,128)(2,1)S(1)}, bf16[512,384]{0,1:T(8,128)(2,1)}, u32[]{:S(2)}) copy-start(bf16[512,384]{0,1:T(8,128)(2,1)} %copy.36) | copy-start | bytes 1179652
  99.6 7.1 %collective-permute-start.8 = (bf16[3,1,16,128]{3,2,1,0:T(8,128)(2,1)S(1)}, bf16[3,1,16,128]{3,2,1,0:T(8,128)(2,1)S(1)}, u32[]{:S(2)}, u32[]{:S(2)}) collective-permute-start(bf16[3,1,16,128]{3,2,1,0:T(8,128)(2,1)S(1)} %get-tuple-element.121), channel_id=1, source_target_pairs={{0,4},{4,8},{8,12},{1,5},{5,9},{9,13},{2,6},{6,10},{10,14},{3,7},{... | collective-permute-start | bytes 36872 | tf_op jit(solution)/shard_map/ppermute | solution.py:15
  101.5 5.2 %collective-permute-start.9 = (bf16[3,1,16,128]{3,2,1,0:T(8,128)(2,1)S(1)}, bf16[3,1,16,128]{3,2,1,0:T(8,128)(2,1)S(1)}, u32[]{:S(2)}, u32[]{:S(2)}) collective-permute-start(bf16[3,1,16,128]{3,2,1,0:T(8,128)(2,1)S(1)} %get-tuple-element.120), channel_id=1, source_target_pairs={{4,0},{8,4},{12,8},{5,1},{9,5},{13,9},{6,2},{10,6},{14,10},{7,3},{... | collective-permute-start | bytes 36872 | tf_op jit(solution)/shard_map/ppermute | solution.py:17
  106.8 6.2 %collective-permute-start.10 = (bf16[3,34,1,128]{3,2,1,0:T(2,128)(2,1)S(1)}, bf16[3,34,1,128]{3,2,1,0:T(2,128)(2,1)S(1)}, u32[]{:S(2)}, u32[]{:S(2)}) collective-permute-start(bf16[3,34,1,128]{3,2,1,0:T(2,128)(2,1)S(1)} %get-tuple-element.112), channel_id=1, source_target_pairs={{0,1},{1,2},{2,3},{4,5},{5,6},{6,7},{8,9},{9,10},{10,11},{12,13},{... | collective-permute-start | bytes 78344 | tf_op jit(solution)/shard_map/ppermute | solution.py:15
  110.3 6.0 %collective-permute-start.11 = (bf16[3,34,1,128]{3,2,1,0:T(2,128)(2,1)S(1)}, bf16[3,34,1,128]{3,2,1,0:T(2,128)(2,1)S(1)}, u32[]{:S(2)}, u32[]{:S(2)}) collective-permute-start(bf16[3,34,1,128]{3,2,1,0:T(2,128)(2,1)S(1)} %get-tuple-element.113), channel_id=1, source_target_pairs={{1,0},{2,1},{3,2},{5,4},{6,5},{7,6},{9,8},{10,9},{11,10},{13,12},{... | collective-permute-start | bytes 78344 | tf_op jit(solution)/shard_map/ppermute | solution.py:17
  118.9 1.5 copy-start.45
  256.7 3.0 %copy-start.12 = (f32[3,3,3,128,128]{4,3,2,1,0:T(8,128)S(1)}, f32[3,3,3,128,128]{4,3,2,1,0:T(8,128)}, u32[]{:S(2)}) copy-start(f32[3,3,3,128,128]{4,3,2,1,0:T(8,128)} %get-tuple-element.3) | copy-start | bytes 5308420
  (29 other events, 31.1 us)
Sparse Core Ops, SparseCore 0:
  113.1 143.4 all-reduce.2
where the time goes:
time: 269 us; the launch traced here: 268 us
  waiting for transfers between devices  150 us (56%)
  local copies, waits for them, and re-layouts  41.2 us (15%)
  starting transfers between devices  25.3 us (9%)
  other arithmetic  18.6 us (7%)
  matrix products  17.8 us (7%)
  between operations  15.4 us (6%)
    psum x1, waiting for transfers between devices, body(): summed_one, summed_two = lax.psum((part_one, part_two), ('ta', 'ha', 'wa'))  134 us
    reshape x18, local copies, waits for them, and re-layouts, window_rows(): return jnp.concatenate(pieces, axis=-1).reshape(-1, 3 * chans)  22.8 us
    ppermute x6, starting transfers between devices, padded_2(): lax.ppermute(tail, axis, [(i, (i + 1) % count) for i in range(ends)])  17.3 us
    ppermute x6, waiting for transfers between devices, padded_2(): lax.ppermute(head, axis, [((i + 1) % count, i) for i in range(ends)])  15.2 us
    dot_general x27, matrix products, conv_local(): jnp.dot(rows, kernel[offset_t, offset_h].reshape(3 * chans, chans), prefe...  13.1 us
    concatenate x16, other arithmetic, window_rows(): return jnp.concatenate(pieces, axis=-1).reshape(-1, 3 * chans)  10.8 us
    ppermute x6, starting transfers between devices, padded_2(): lax.ppermute(head, axis, [((i + 1) % count, i) for i in range(ends)])  7.93 us
    unnamed x130, local copies, waits for them, and re-layouts  6.02 us
  transfers between devices with their start and end apart: 13, of which 6 were waited for; matrix products, arithmetic and copies ran while one was open for 7% of the time, Pallas kernels for 0%

commit v1 on v0

--- a/solution.py
+++ b/solution.py
@@ -1,7 +1,213 @@
+import functools
+
 import jax
 import jax.numpy as jnp
 from jax import lax
+from jax.experimental import pallas as pl
+from jax.experimental.pallas import tpu as pltpu
 from jax.sharding import PartitionSpec as P
+
+MESH = pl.DeviceIdType.MESH
+TILE = 16
+
+
+class Sizes:
+    def __init__(self, mesh):
+        self.nt, self.nh, self.nw = mesh.shape["ta"], mesh.shape["ha"], mesh.shape["wa"]
+        self.cores = 2 if self.nh % 2 == 0 else 1
+        self.rows = self.nh // self.cores
+        self.plane = self.nt * self.rows
+        self.devices = self.nt * self.nh * self.nw
+
+
+def chunks_of(total, devices, pieces):
+    units = -(-total // devices)
+    pieces = min(pieces, units)
+    cuts = [units * i // pieces for i in range(pieces + 1)]
+    return [(a * devices, (b - a) * devices) for a, b in zip(cuts, cuts[1:])]
+
+
+class Reduce:
+    def __init__(self, sizes, where, source, out, first, tiles, base, bufs, send, recv, sem):
+        self.s, self.source, self.out = sizes, source, out
+        self.ti, self.hi, self.wi = where
+        self.core = self.hi % sizes.cores
+        self.half = tiles // sizes.cores
+        self.part = self.half // sizes.plane
+        self.shard = self.part // sizes.nw
+        self.me = self.ti * sizes.rows + self.hi // sizes.cores
+        self.first, self.base = first, base
+        self.land_core, self.land_plane, self.land_wa, self.acc = bufs
+        self.send, self.recv, self.sem = send, recv, sem
+        self.open = []
+
+    def copy(self, src, dst, device):
+        made = pltpu.make_async_remote_copy(
+            src_ref=src, dst_ref=dst, send_sem=self.send.at[self.sem], recv_sem=self.recv.at[self.sem],
+            device_id=device, device_id_type=MESH,
+        )
+        self.sem += 1
+        made.start()
+        self.open.append(made)
+        return made
+
+    def core_device(self):
+        return (self.ti, self.hi + 1 - 2 * self.core, self.wi)
+
+    def plane_device(self, step):
+        to = lax.rem(self.me + step, self.s.plane)
+        return to, (to // self.s.rows, (to % self.s.rows) * self.s.cores + self.core, self.wi)
+
+    def wa_device(self, step):
+        to = lax.rem(self.wi + step, self.s.nw)
+        return to, (self.ti, self.hi, to)
+
+    def start_core(self):
+        s = self.s
+        self.waits = []
+        if s.cores == 2:
+            other = self.source.at[pl.ds(self.first + (1 - self.core) * self.half, self.half)]
+            land = self.land_core.at[pl.ds(self.base // 2, self.half)]
+            self.waits = [self.copy(other, land, self.core_device())]
+
+    def start_plane(self):
+        s = self.s
+        for made in self.waits:
+            made.wait_recv()
+        mine = self.source[pl.ds(self.first + self.core * self.half, self.half)]
+        at = self.base // s.cores
+        if s.cores == 2:
+            mine = mine.astype(jnp.float32) + self.land_core[pl.ds(at, self.half)].astype(jnp.float32)
+        self.acc[pl.ds(at, self.half)] = mine.astype(jnp.bfloat16)
+        self.waits = []
+        for step in range(1, s.plane):
+            to, device = self.plane_device(step)
+            src = self.acc.at[pl.ds(at + to * self.part, self.part)]
+            dst = self.land_plane.at[step - 1, pl.ds(at // s.plane, self.part)]
+            self.waits.append(self.copy(src, dst, device))
+
+    def start_wa(self):
+        s = self.s
+        for made in self.waits:
+            made.wait_recv()
+        at = self.base // s.cores
+        low = at // s.plane
+        total = self.acc[pl.ds(at + self.me * self.part, self.part)].astype(jnp.float32)
+        for step in range(1, s.plane):
+            total = total + self.land_plane[step - 1, pl.ds(low, self.part)].astype(jnp.float32)
+        spare = self.land_plane.at[s.plane - 1]
+        spare[pl.ds(low, self.part)] = total.astype(jnp.bfloat16)
+        self.waits = []
+        for step in range(1, s.nw):
+            to, device = self.wa_device(step)
+            src = spare.at[pl.ds(low + to * self.shard, self.shard)]
+            dst = self.land_wa.at[step - 1, pl.ds(low // s.nw, self.shard)]
+            self.waits.append(self.copy(src, dst, device))
+
+    def back_wa(self):
+        s = self.s
+        for made in self.waits:
+            made.wait_recv()
+        low = self.base // s.cores // s.plane
+        spare = self.land_plane.at[s.plane - 1]
+        total = spare[pl.ds(low + self.wi * self.shard, self.shard)].astype(jnp.float32)
+        for step in range(1, s.nw):
+            total = total + self.land_wa[step - 1, pl.ds(low // s.nw, self.shard)].astype(jnp.float32)
+        here = self.first + self.core * self.half + self.me * self.part
+        mine = self.out.at[pl.ds(here + self.wi * self.shard, self.shard)]
+        mine[...] = total.astype(jnp.bfloat16)
+        self.waits = [self.copy(mine, mine, self.wa_device(step)[1]) for step in range(1, s.nw)]
+
+    def back_plane(self):
+        s = self.s
+        for made in self.waits:
+            made.wait_recv()
+        here = self.first + self.core * self.half + self.me * self.part
+        mine = self.out.at[pl.ds(here, self.part)]
+        self.waits = [self.copy(mine, mine, self.plane_device(step)[1]) for step in range(1, s.plane)]
+
+    def back_core(self):
+        for made in self.waits:
+            made.wait_recv()
+        self.waits = []
+        if self.s.cores == 2:
+            mine = self.out.at[pl.ds(self.first + self.core * self.half, self.half)]
+            self.waits = [self.copy(mine, mine, self.core_device())]
+
+    def finish(self):
+        for made in self.waits:
+            made.wait_recv()
+        for made in self.open:
+            made.wait_send()
+
+
+def copies_of(sizes):
+    return 2 * ((sizes.cores - 1) + (sizes.plane - 1) + (sizes.nw - 1))
+
+
+STAGES = ("start_core", "start_plane", "start_wa", "back_wa", "back_plane", "back_core", "finish")
+
+
+def reduce_scratch(sizes, tiles, count):
+    half = tiles // sizes.cores
+    part = half // sizes.plane
+    return [
+        pltpu.VMEM((half, TILE, 128), jnp.bfloat16),
+        pltpu.VMEM((sizes.plane, part, TILE, 128), jnp.bfloat16),
+        pltpu.VMEM((max(sizes.nw - 1, 1), part // sizes.nw, TILE, 128), jnp.bfloat16),
+        pltpu.VMEM((half, TILE, 128), jnp.bfloat16),
+        pltpu.SemaphoreType.DMA((count * copies_of(sizes),)),
+        pltpu.SemaphoreType.DMA((count * copies_of(sizes),)),
+    ]
+
+
+def reduce_partners(sizes, where):
+    ti, hi, wi = where
+    core = hi % sizes.cores
+    me = ti * sizes.rows + hi // sizes.cores
+    found = []
+    if sizes.cores == 2:
+        found.append((ti, hi + 1 - 2 * core, wi))
+    for step in range(1, sizes.plane):
+        to = lax.rem(me + step, sizes.plane)
+        found.append((to // sizes.rows, (to % sizes.rows) * sizes.cores + core, wi))
+    for step in range(1, sizes.nw):
+        found.append((ti, hi, lax.rem(wi + step, sizes.nw)))
+    return found
+
+
+def reduce_kernel(sizes, ranges, part_ref, out_ref, *scratch):
+    bufs, (send, recv) = scratch[:4], scratch[4:]
+    where = (lax.axis_index("ta"), lax.axis_index("ha"), lax.axis_index("wa"))
+    partners = reduce_partners(sizes, where)
+    barrier = pltpu.get_barrier_semaphore()
+    for device in partners:
+        pl.semaphore_signal(barrier, inc=1, device_id=device, device_id_type=MESH)
+    pl.semaphore_wait(barrier, len(partners))
+    runs = [
+        Reduce(sizes, where, part_ref, out_ref, first, tiles, first, bufs, send, recv, i * copies_of(sizes))
+        for i, (first, tiles) in enumerate(ranges)
+    ]
+    for stage in STAGES:
+        for run in runs:
+            getattr(run, stage)()
+
+
+def all_sum(sizes, parts, pieces):
+    total = parts.shape[0]
+    ranges = chunks_of(total, sizes.devices, pieces)
+    tiles = sum(size for _, size in ranges)
+    parts = jnp.pad(parts, ((0, tiles - total), (0, 0), (0, 0)))
+    return pl.pallas_call(
+        functools.partial(reduce_kernel, sizes, ranges),
+        out_shape=jax.ShapeDtypeStruct((tiles, TILE, 128), jnp.bfloat16),
+        in_specs=[pl.BlockSpec(memory_space=pltpu.VMEM)],
+        out_specs=pl.BlockSpec(memory_space=pltpu.VMEM),
+        scratch_shapes=reduce_scratch(sizes, tiles, len(ranges)),
+        compiler_params=pltpu.CompilerParams(
+            collective_id=0, has_side_effects=True, vmem_limit_bytes=48 * 1024 * 1024
+        ),
+    )(parts)[:total]
 
 
 def padded_2(cells, sides, width):
@@ -68,7 +274,7 @@
     return jnp.stack(blocks).reshape(3, 3, 3, chans, chans)
 
 
-def body(volume, cotangent, kernel_one, kernel_two):
+def body(sizes, volume, cotangent, kernel_one, kernel_two):
     stacked = jnp.stack((volume, cotangent))
     padded_both = padded_2(stacked, (("ta", 1), ("ha", 2), ("wa", 3)), 1)
     volume_pad = padded_both[0]
@@ -91,11 +297,14 @@
     d_pre_pad = padded_2(d_pre, (("ta", 0), ("ha", 1), ("wa", 2)), 1)
     d_volume = conv_local(d_pre_pad, flip_swap(kernel_one)).astype(jnp.bfloat16)
     part_one = kernel_local(volume_pad, d_pre)
-    summed_one, summed_two = lax.psum((part_one, part_two), ("ta", "ha", "wa"))
-    return (d_volume, summed_one * scale, summed_two * scale)
+    both = jnp.concatenate([part_one.reshape(-1), part_two.reshape(-1)]).astype(jnp.bfloat16)
+    summed = all_sum(sizes, both.reshape(-1, TILE, 128), 4).reshape((2,) + kernel_one.shape)
+    summed = summed.astype(jnp.float32) * scale
+    return (d_volume, summed[0], summed[1])
 
 
 def solution(mesh):
     in_specs = (P("ta", "ha", "wa", None), P("ta", "ha", "wa", None), P(), P())
     out_specs = (P("ta", "ha", "wa", None), P(), P())
-    return jax.shard_map(body, mesh=mesh, in_specs=in_specs, out_specs=out_specs, check_vma=False)
+    return jax.shard_map(
+        functools.partial(body, Sizes(mesh)), mesh=mesh, in_specs=in_specs, out_specs=out_specs, check_vma=False)

time: 269 us -> 153 us (0.57)
  waiting for transfers between devices: 150 us -> 15.1 us
  Pallas kernels: 0 us -> 37.2 us
  between operations: 15.4 us -> 1.84 us
  other arithmetic: 18.6 us -> 14.9 us
    psum x1 -> x0, waiting for transfers between devices: 134 us -> none  [body(): summed_one, summed_two = lax.psum((part_one, part_two), ('ta', 'ha', 'wa'))]
    pallas_call x0 -> x1, Pallas kernels: none -> 37.2 us  [all_sum(): pl.pallas_call(functools.partial(reduce_kernel, sizes, ranges), out_shape...]
    mul x2 -> x1, other arithmetic: 4.39 us -> 0.23 us  [body(): summed = summed.astype(jnp.float32) * scale]
    unnamed x130 -> x110, local copies, waits for them, and re-layouts: 6.02 us -> 4.81 us
  transfers between devices with their start and end apart: 13 -> 12, of which waited for: 6 -> 5; matrix products, arithmetic and copies ran while one was open for 7% -> 11% of each run, Pallas kernels for 0% -> 25%
where the time goes in v1:
time: 153 us; the launch traced here: 152 us
  local copies, waits for them, and re-layouts  39.5 us (26%)
  Pallas kernels  37.2 us (24%)
  starting transfers between devices  24.9 us (16%)
  matrix products  18.2 us (12%)
  waiting for transfers between devices  15.1 us (10%)
  other arithmetic  14.9 us (10%)
  between operations  1.84 us (1%)
    pallas_call x1, Pallas kernels, all_sum(): pl.pallas_call(functools.partial(reduce_kernel, sizes, ranges), out_shape...  37.2 us
    reshape x18, local copies, waits for them, and re-layouts, window_rows(): return jnp.concatenate(pieces, axis=-1).reshape(-1, 3 * chans)  22.9 us
    ppermute x6, starting transfers between devices, padded_2(): lax.ppermute(tail, axis, [(i, (i + 1) % count) for i in range(ends)])  17 us
    ppermute x6, waiting for transfers between devices, padded_2(): lax.ppermute(head, axis, [((i + 1) % count, i) for i in range(ends)])  15.1 us
    dot_general x27, matrix products, conv_local(): jnp.dot(rows, kernel[offset_t, offset_h].reshape(3 * chans, chans), prefe...  13 us
    concatenate x16, other arithmetic, window_rows(): return jnp.concatenate(pieces, axis=-1).reshape(-1, 3 * chans)  10.9 us
    ppermute x6, starting transfers between devices, padded_2(): lax.ppermute(head, axis, [((i + 1) % count, i) for i in range(ends)])  7.93 us
    dot_general x18, matrix products, kernel_local(): lax.dot_general(rows, right, (((0,), (0,)), ((), ())), preferred_element_...  5.15 us
  transfers between devices with their start and end apart: 12, of which 5 were waited for; matrix products, arithmetic and copies ran while one was open for 11% of the time, Pallas kernels for 25%

profile of v1, /device:TPU:0, one launch (start us, length us, event | category | flops | bytes accessed | tf_op | source)
XLA Modules:
  0.0 151.6 jit_solution(8543671234883740994)
XLA Ops:
  0.6 1.8 %pad_maximum_fusion.40 = bf16[2,1,32,16,128]{4,3,2,1,0:T(8,128)(2,1)} fusion(bf16[1,1,32,16,128]{4,3,2,1,0:T(8,128)(2,1)} %bitcast.345, bf16[1,1,32,16,128]{4,3,2,1,0:T(8,128)(2,1)} %bitcast.349), kind=kLoop, calls=%fused_computation.138 | loop fusion | flops 131072 | bytes 524288 | tf_op jit(solution)/shard_map/stack | solution.py:278
  2.4 4.9 %collective-permute-start = (bf16[2,1,32,16,128]{4,3,2,1,0:T(8,128)(2,1)}, bf16[2,1,32,16,128]{4,3,2,1,0:T(8,128)(2,1)S(1)}, u32[]{:S(2)}, u32[]{:S(2)}) collective-permute-start(bf16[2,1,32,16,128]{4,3,2,1,0:T(8,128)(2,1)} %pad_maximum_fusion.40), channel_id=1, source_target_pairs={{0,16},{1,17},{2,18},{3,19},{4,20},{5,21},{6,22},{7,23},{8,24},{9,... | collective-permute-start | bytes 786440 | tf_op jit(solution)/shard_map/ppermute | solution.py:221
  7.3 1.3 collective-permute-start.1
  8.6 2.2 %fusion.70 = (bf16[1,1,3,128,128]{4,3,2,1,0:T(8,128)(2,1)}, bf16[1,1,3,128,128]{4,3,2,1,0:T(8,128)(2,1)}, bf16[1,1,3,128,128]{4,3,2,1,0:T(8,128)(2,1)}, bf16[1,1...) fusion(bf16[3,3,3,128,128]{4,3,2,1,0:T(8,128)(2,1)} %param.6), kind=kLoop, calls=%fused_computation.183 | loop fusion | bytes 1769472 | tf_op jit(solution)/shard_map/slice | solution.py:257
  10.8 1.4 copy.26
  12.3 1.4 copy.27
  13.7 1.0 fusion.69
  14.7 2.5 %collective-permute-done.1 = bf16[2,1,32,16,128]{4,3,2,1,0:T(8,128)(2,1)S(1)} collective-permute-done((bf16[2,1,32,16,128]{4,3,2,1,0:T(8,128)(2,1)}, bf16[2,1,32,16,128]{4,3,2,1,0:T(8,128)(2,1)S(1)}, u32[]{:S(2)}, u32[]{:S(2)}) %collective-permute-start.1) | collective-permute-done | bytes 262176 | tf_op jit(solution)/shard_map/ppermute | solution.py:223
  17.2 1.3 collective-permute-start.2
  18.5 1.3 collective-permute-start.3
  19.9 3.4 %collective-permute-done.3 = bf16[2,3,1,16,128]{4,3,2,1,0:T(8,128)(2,1)S(1)} collective-permute-done((bf16[2,3,1,16,128]{4,3,2,1,0:T(8,128)(2,1)S(1)}, bf16[2,3,1,16,128]{4,3,2,1,0:T(8,128)(2,1)S(1)}, u32[]{:S(2)}, u32[]{:S(2)}) %collective-permute-start.3) | collective-permute-done | bytes 24608 | tf_op jit(solution)/shard_map/ppermute | solution.py:223
  23.5 3.5 %collective-permute-start.4 = (bf16[2,3,34,1,128]{4,3,2,1,0:T(2,128)(2,1)S(1)}, bf16[2,3,34,1,128]{4,3,2,1,0:T(2,128)(2,1)S(1)}, u32[]{:S(2)}, u32[]{:S(2)}) collective-permute-start(bf16[2,3,34,1,128]{4,3,2,1,0:T(2,128)(2,1)S(1)} %get-tuple-element.34), channel_id=1, source_target_pairs={{0,1},{1,2},{2,3},{4,5},{5,6},{6,7},{8,9},{9,10},{10,11},{12,13},{... | collective-permute-start | bytes 156680 | tf_op jit(solution)/shard_map/ppermute | solution.py:221
  27.0 1.3 collective-permute-start.5
  29.2 4.3 %collective-permute-done.5 = bf16[2,3,34,1,128]{4,3,2,1,0:T(2,128)(2,1)S(1)} collective-permute-done((bf16[2,3,34,1,128]{4,3,2,1,0:T(2,128)(2,1)S(1)}, bf16[2,3,34,1,128]{4,3,2,1,0:T(2,128)(2,1)S(1)}, u32[]{:S(2)}, u32[]{:S(2)}) %collective-permute-start.5) | collective-permute-done | bytes 52256 | tf_op jit(solution)/shard_map/ppermute | solution.py:223
  34.6 1.0 fusion.75
  35.6 1.0 fusion.74
  36.6 1.5 fusion.73
  39.1 1.9 %fusion.78 = f32[512,128]{1,0:T(8,128)} fusion(bf16[512,384]{1,0:T(8,128)(2,1)S(1)} %bitcast.320, bf16[384,128]{1,0:T(8,128)(2,1)} %bitcast.388), kind=kOutput, calls=%fused_computation.191 | convolution fusion | flops 50331648 | bytes 753664 | tf_op jit(solution)/shard_map/dot_general | solution.py:255
  41.9 1.9 %fusion.77 = f32[512,128]{1,0:T(8,128)} fusion(bf16[512,384]{1,0:T(8,128)(2,1)S(1)} %bitcast.322, bf16[384,128]{1,0:T(8,128)(2,1)} %bitcast.389), kind=kOutput, calls=%fused_computation.190 | convolution fusion | flops 50331648 | bytes 753664 | tf_op jit(solution)/shard_map/dot_general | solution.py:255
  46.8 1.0 copy.32
  47.9 0.9 copy.33
  48.8 0.9 copy.34
  49.8 1.1 pad_maximum_fusion.36
  52.8 1.1 pad_maximum_fusion.21
  54.8 1.1 pad_maximum_fusion.22
  55.9 0.9 copy.39
  56.9 2.2 %pad_maximum_fusion.23 = (bf16[1,32,16,384]{3,2,1,0:T(8,128)(2,1)}, bf16[1,32,16,384]{3,2,1,0:T(8,128)(2,1)}) fusion(bf16[1,32,16,128]{3,2,1,0:T(8,128)(2,1)} %get-tuple-element.71, bf16[1,32,16,128]{3,2,1,0:T(8,128)(2,1)} %get-tuple-element.72, bf16[1,32,16,128]{3,2,1,0:T(8,128)(2,1)} %get-tuple-element.73, bf16[1,32,16,128]{3,2,1,0:T(8,128)(2,1)} %get-tuple-element.68, ...), kind=kLoop, calls=%fused_computation.116 | loop fusion | flops 2359296 | bytes 1572864 | tf_op jit(solution)/shard_map/concatenate | solution.py:243
  59.1 1.9 %copy.40 = bf16[512,384]{0,1:T(8,128)(2,1)} copy(bf16[512,384]{1,0:T(8,128)(2,1)} %bitcast.335) | data formatting | bytes 786432 | tf_op jit(solution)/shard_map/reshape | solution.py:243
  61.0 1.9 %copy.41 = bf16[512,384]{0,1:T(8,128)(2,1)} copy(bf16[512,384]{1,0:T(8,128)(2,1)} %bitcast.333) | data formatting | bytes 786432 | tf_op jit(solution)/shard_map/reshape | solution.py:243
  62.9 2.3 %pad_maximum_fusion.25 = (bf16[1,32,16,384]{3,2,1,0:T(8,128)(2,1)}, bf16[1,32,16,384]{3,2,1,0:T(8,128)(2,1)}) fusion(bf16[1,32,16,128]{3,2,1,0:T(8,128)(2,1)} %get-tuple-element.65, bf16[1,32,16,128]{3,2,1,0:T(8,128)(2,1)} %get-tuple-element.66, bf16[1,32,16,128]{3,2,1,0:T(8,128)(2,1)} %get-tuple-element.67, bf16[1,32,16,128]{3,2,1,0:T(8,128)(2,1)} %get-tuple-element.62, ...), kind=kLoop, calls=%fused_computation.118 | loop fusion | flops 2359296 | bytes 1572864 | tf_op jit(solution)/shard_map/concatenate | solution.py:243
  65.2 1.9 %copy.42 = bf16[512,384]{0,1:T(8,128)(2,1)} copy(bf16[512,384]{1,0:T(8,128)(2,1)} %bitcast.339) | data formatting | bytes 786432 | tf_op jit(solution)/shard_map/reshape | solution.py:243
  67.1 1.9 %copy.43 = bf16[512,384]{0,1:T(8,128)(2,1)} copy(bf16[512,384]{1,0:T(8,128)(2,1)} %bitcast.337) | data formatting | bytes 786432 | tf_op jit(solution)/shard_map/reshape | solution.py:243
  69.0 2.2 %pad_maximum_fusion.27 = (bf16[1,32,16,384]{3,2,1,0:T(8,128)(2,1)}, bf16[1,32,16,384]{3,2,1,0:T(8,128)(2,1)}) fusion(bf16[1,32,16,128]{3,2,1,0:T(8,128)(2,1)} %get-tuple-element.59, bf16[1,32,16,128]{3,2,1,0:T(8,128)(2,1)} %get-tuple-element.60, bf16[1,32,16,128]{3,2,1,0:T(8,128)(2,1)} %get-tuple-element.61, bf16[1,32,16,128]{3,2,1,0:T(8,128)(2,1)} %get-tuple-element.57, ...), kind=kLoop, calls=%fused_computation.120 | loop fusion | flops 2359296 | bytes 1572864 | tf_op jit(solution)/shard_map/concatenate | solution.py:243
  71.2 2.0 %copy.44 = bf16[512,384]{0,1:T(8,128)(2,1)} copy(bf16[512,384]{1,0:T(8,128)(2,1)} %bitcast.343) | data formatting | bytes 786432 | tf_op jit(solution)/shard_map/reshape | solution.py:243
  73.2 1.9 %copy.45 = bf16[512,384]{0,1:T(8,128)(2,1)} copy(bf16[512,384]{1,0:T(8,128)(2,1)} %bitcast.341) | data formatting | bytes 786432 | tf_op jit(solution)/shard_map/reshape | solution.py:243
  75.1 1.3 convolution_add_fusion.15
  76.5 1.2 convolution_add_fusion.14
  82.4 2.3 %collective-permute-start.6 = (bf16[1,32,16,128]{3,2,1,0:T(8,128)(2,1)S(1)}, bf16[1,32,16,128]{3,2,1,0:T(8,128)(2,1)S(1)}, u32[]{:S(2)}, u32[]{:S(2)}) collective-permute-start(bf16[1,32,16,128]{3,2,1,0:T(8,128)(2,1)S(1)} %multiply_convert_fusion.2), channel_id=1, source_target_pairs={{0,16},{1,17},{2,18},{3,19},{4,20},{5,21},{6,22},{7,23},{8,24},{9,... | collective-permute-start | bytes 393224 | tf_op jit(solution)/shard_map/ppermute | solution.py:221
  84.7 1.5 collective-permute-start.7
  89.0 1.4 copy.46
  93.8 37.2 %shard_map.67 = bf16[448,16,128]{2,1,0:T(8,128)(2,1)S(1)} custom-call(bf16[448,16,128]{2,1,0:T(8,128)(2,1)S(1)} %fusion.2.part_ref), custom_call_target="tpu_custom_call" | custom-call | tf_op jit(solution)/shard_map/pallas_call | solution.py:201
  131.0 2.3 %collective-permute-start.8 = (bf16[3,1,16,128]{3,2,1,0:T(8,128)(2,1)S(1)}, bf16[3,1,16,128]{3,2,1,0:T(8,128)(2,1)S(1)}, u32[]{:S(2)}, u32[]{:S(2)}) collective-permute-start(bf16[3,1,16,128]{3,2,1,0:T(8,128)(2,1)S(1)} %get-tuple-element.121), channel_id=1, source_target_pairs={{0,4},{4,8},{8,12},{1,5},{5,9},{9,13},{2,6},{6,10},{10,14},{3,7},{... | collective-permute-start | bytes 36872 | tf_op jit(solution)/shard_map/ppermute | solution.py:221
  133.3 1.3 collective-permute-start.9
  134.9 2.1 %collective-permute-done.9 = bf16[3,1,16,128]{3,2,1,0:T(8,128)(2,1)S(1)} collective-permute-done((bf16[3,1,16,128]{3,2,1,0:T(8,128)(2,1)S(1)}, bf16[3,1,16,128]{3,2,1,0:T(8,128)(2,1)S(1)}, u32[]{:S(2)}, u32[]{:S(2)}) %collective-permute-start.9) | collective-permute-done | bytes 12320 | tf_op jit(solution)/shard_map/ppermute | solution.py:223
  137.1 2.7 %collective-permute-start.10 = (bf16[3,34,1,128]{3,2,1,0:T(2,128)(2,1)S(1)}, bf16[3,34,1,128]{3,2,1,0:T(2,128)(2,1)S(1)}, u32[]{:S(2)}, u32[]{:S(2)}) collective-permute-start(bf16[3,34,1,128]{3,2,1,0:T(2,128)(2,1)S(1)} %get-tuple-element.112), channel_id=1, source_target_pairs={{0,1},{1,2},{2,3},{4,5},{5,6},{6,7},{8,9},{9,10},{10,11},{12,13},{... | collective-permute-start | bytes 78344 | tf_op jit(solution)/shard_map/ppermute | solution.py:221
  139.9 1.3 collective-permute-start.11
  141.2 2.0 %fusion.67 = (f32[216,16,128]{2,1,0:T(8,128)}, f32[216,16,128]{2,1,0:T(8,128)}) fusion(f32[432,16,128]{2,1,0:T(8,128)S(1)} %convert_multiply_fusion), kind=kLoop, calls=%fused_computation.180 | loop fusion | bytes 7077888 | tf_op jit(solution)/shard_map/slice | solution.py:303
  143.2 2.7 %collective-permute-done.11 = bf16[3,34,1,128]{3,2,1,0:T(2,128)(2,1)S(1)} collective-permute-done((bf16[3,34,1,128]{3,2,1,0:T(2,128)(2,1)S(1)}, bf16[3,34,1,128]{3,2,1,0:T(2,128)(2,1)S(1)}, u32[]{:S(2)}, u32[]{:S(2)}) %collective-permute-start.11) | collective-permute-done | bytes 26144 | tf_op jit(solution)/shard_map/ppermute | solution.py:223
  (190 shorter events, 26.4 us)
Async XLA Ops:
  0.6 10.2 %copy-start.30 = (bf16[3,3,3,128,128]{4,3,2,1,0:T(8,128)(2,1)S(1)}, bf16[3,3,3,128,128]{4,3,2,1,0:T(8,128)(2,1)}, u32[]{:S(2)}) copy-start(bf16[3,3,3,128,128]{4,3,2,1,0:T(8,128)(2,1)} %param.7) | copy-start | bytes 2654212
  2.4 12.3 %collective-permute-start = (bf16[2,1,32,16,128]{4,3,2,1,0:T(8,128)(2,1)}, bf16[2,1,32,16,128]{4,3,2,1,0:T(8,128)(2,1)S(1)}, u32[]{:S(2)}, u32[]{:S(2)}) collective-permute-start(bf16[2,1,32,16,128]{4,3,2,1,0:T(8,128)(2,1)} %pad_maximum_fusion.40), channel_id=1, source_target_pairs={{0,16},{1,17},{2,18},{3,19},{4,20},{5,21},{6,22},{7,23},{8,24},{9,... | collective-permute-start | bytes 786440 | tf_op jit(solution)/shard_map/ppermute | solution.py:221
  7.3 9.9 %collective-permute-start.1 = (bf16[2,1,32,16,128]{4,3,2,1,0:T(8,128)(2,1)}, bf16[2,1,32,16,128]{4,3,2,1,0:T(8,128)(2,1)S(1)}, u32[]{:S(2)}, u32[]{:S(2)}) collective-permute-start(bf16[2,1,32,16,128]{4,3,2,1,0:T(8,128)(2,1)} %pad_maximum_fusion.40), channel_id=1, source_target_pairs={{16,0},{17,1},{18,2},{19,3},{20,4},{21,5},{22,6},{23,7},{24,8},{25... | collective-permute-start | bytes 786440 | tf_op jit(solution)/shard_map/ppermute | solution.py:223
  10.8 1.5 copy-start
  12.3 4.9 %copy-start.7 = (bf16[1,32,16,128]{3,2,1,0:T(8,128)(2,1)S(1)}, bf16[1,32,16,128]{3,2,1,0:T(8,128)(2,1)}, u32[]{:S(2)}) copy-start(bf16[1,32,16,128]{3,2,1,0:T(8,128)(2,1)} %param.5) | copy-start | bytes 393220
  12.3 4.8 %copy-start.8 = (bf16[1,32,16,128]{3,2,1,0:T(8,128)(2,1)S(1)}, bf16[1,32,16,128]{3,2,1,0:T(8,128)(2,1)}, u32[]{:S(2)}) copy-start(bf16[1,32,16,128]{3,2,1,0:T(8,128)(2,1)} %param.4) | copy-start | bytes 393220
  17.2 2.7 %collective-permute-start.2 = (bf16[2,3,1,16,128]{4,3,2,1,0:T(8,128)(2,1)S(1)}, bf16[2,3,1,16,128]{4,3,2,1,0:T(8,128)(2,1)S(1)}, u32[]{:S(2)}, u32[]{:S(2)}) collective-permute-start(bf16[2,3,1,16,128]{4,3,2,1,0:T(8,128)(2,1)S(1)} %get-tuple-element.36), channel_id=1, source_target_pairs={{0,4},{4,8},{8,12},{1,5},{5,9},{9,13},{2,6},{6,10},{10,14},{3,7},{... | collective-permute-start | bytes 73736 | tf_op jit(solution)/shard_map/ppermute | solution.py:221
  18.5 4.8 %collective-permute-start.3 = (bf16[2,3,1,16,128]{4,3,2,1,0:T(8,128)(2,1)S(1)}, bf16[2,3,1,16,128]{4,3,2,1,0:T(8,128)(2,1)S(1)}, u32[]{:S(2)}, u32[]{:S(2)}) collective-permute-start(bf16[2,3,1,16,128]{4,3,2,1,0:T(8,128)(2,1)S(1)} %get-tuple-element.37), channel_id=1, source_target_pairs={{4,0},{8,4},{12,8},{5,1},{9,5},{13,9},{6,2},{10,6},{14,10},{7,3},{... | collective-permute-start | bytes 73736 | tf_op jit(solution)/shard_map/ppermute | solution.py:223
  23.5 5.7 %collective-permute-start.4 = (bf16[2,3,34,1,128]{4,3,2,1,0:T(2,128)(2,1)S(1)}, bf16[2,3,34,1,128]{4,3,2,1,0:T(2,128)(2,1)S(1)}, u32[]{:S(2)}, u32[]{:S(2)}) collective-permute-start(bf16[2,3,34,1,128]{4,3,2,1,0:T(2,128)(2,1)S(1)} %get-tuple-element.34), channel_id=1, source_target_pairs={{0,1},{1,2},{2,3},{4,5},{5,6},{6,7},{8,9},{9,10},{10,11},{12,13},{... | collective-permute-start | bytes 156680 | tf_op jit(solution)/shard_map/ppermute | solution.py:221
  27.0 6.6 %collective-permute-start.5 = (bf16[2,3,34,1,128]{4,3,2,1,0:T(2,128)(2,1)S(1)}, bf16[2,3,34,1,128]{4,3,2,1,0:T(2,128)(2,1)S(1)}, u32[]{:S(2)}, u32[]{:S(2)}) collective-permute-start(bf16[2,3,34,1,128]{4,3,2,1,0:T(2,128)(2,1)S(1)} %get-tuple-element.35), channel_id=1, source_target_pairs={{1,0},{2,1},{3,2},{5,4},{6,5},{7,6},{9,8},{10,9},{11,10},{13,12},{... | collective-permute-start | bytes 156680 | tf_op jit(solution)/shard_map/ppermute | solution.py:223
  50.9 1.9 %copy-start.20 = (bf16[1,32,16,384]{3,2,1,0:T(8,128)(2,1)}, bf16[1,32,16,384]{3,2,1,0:T(8,128)(2,1)S(1)}, u32[]{:S(2)}) copy-start(bf16[1,32,16,384]{3,2,1,0:T(8,128)(2,1)S(1)} %get-tuple-element.144) | copy-start | bytes 1179652
  75.1 2.5 %copy-start.51 = (bf16[1,1,3,128,128]{4,3,2,1,0:T(8,128)(2,1)S(1)}, bf16[1,1,3,128,128]{4,3,2,1,0:T(8,128)(2,1)}, u32[]{:S(2)}) copy-start(bf16[1,1,3,128,128]{4,3,2,1,0:T(8,128)(2,1)} %get-tuple-element.30) | copy-start | bytes 294916
  75.1 2.8 %copy-start.50 = (bf16[1,1,3,128,128]{4,3,2,1,0:T(8,128)(2,1)S(1)}, bf16[1,1,3,128,128]{4,3,2,1,0:T(8,128)(2,1)}, u32[]{:S(2)}) copy-start(bf16[1,1,3,128,128]{4,3,2,1,0:T(8,128)(2,1)} %get-tuple-element.29) | copy-start | bytes 294916
  76.4 1.8 %copy-start.49 = (bf16[1,1,3,128,128]{4,3,2,1,0:T(8,128)(2,1)S(1)}, bf16[1,1,3,128,128]{4,3,2,1,0:T(8,128)(2,1)}, u32[]{:S(2)}) copy-start(bf16[1,1,3,128,128]{4,3,2,1,0:T(8,128)(2,1)} %get-tuple-element.28) | copy-start | bytes 294916
  79.8 1.1 copy-start.3
  79.8 1.1 copy-start.41
  80.2 1.1 copy-start.6
  80.2 1.1 copy-start.40
  80.5 1.1 copy-start.5
  80.5 1.1 copy-start.39
  80.9 1.1 copy-start.21
  80.9 1.1 copy-start.53
  81.6 4.6 %copy-start.18 = (bf16[512,384]{0,1:T(8,128)(2,1)S(1)}, bf16[512,384]{0,1:T(8,128)(2,1)}, u32[]{:S(2)}) copy-start(bf16[512,384]{0,1:T(8,128)(2,1)} %copy.37) | copy-start | bytes 1179652
  81.9 4.6 %copy-start.19 = (bf16[512,384]{0,1:T(8,128)(2,1)S(1)}, bf16[512,384]{0,1:T(8,128)(2,1)}, u32[]{:S(2)}) copy-start(bf16[512,384]{0,1:T(8,128)(2,1)} %copy.38) | copy-start | bytes 1179652
  82.0 4.8 %copy-start.22 = (bf16[512,384]{0,1:T(8,128)(2,1)S(1)}, bf16[512,384]{0,1:T(8,128)(2,1)}, u32[]{:S(2)}) copy-start(bf16[512,384]{0,1:T(8,128)(2,1)} %copy.39) | copy-start | bytes 1179652
  82.3 4.8 %copy-start.24 = (bf16[512,384]{0,1:T(8,128)(2,1)S(1)}, bf16[512,384]{0,1:T(8,128)(2,1)}, u32[]{:S(2)}) copy-start(bf16[512,384]{0,1:T(8,128)(2,1)} %copy.40) | copy-start | bytes 1179652
  82.3 5.1 %copy-start.23 = (bf16[512,384]{0,1:T(8,128)(2,1)S(1)}, bf16[512,384]{0,1:T(8,128)(2,1)}, u32[]{:S(2)}) copy-start(bf16[512,384]{0,1:T(8,128)(2,1)} %copy.41) | copy-start | bytes 1179652
  82.4 48.5 %collective-permute-start.6 = (bf16[1,32,16,128]{3,2,1,0:T(8,128)(2,1)S(1)}, bf16[1,32,16,128]{3,2,1,0:T(8,128)(2,1)S(1)}, u32[]{:S(2)}, u32[]{:S(2)}) collective-permute-start(bf16[1,32,16,128]{3,2,1,0:T(8,128)(2,1)S(1)} %multiply_convert_fusion.2), channel_id=1, source_target_pairs={{0,16},{1,17},{2,18},{3,19},{4,20},{5,21},{6,22},{7,23},{8,24},{9,... | collective-permute-start | bytes 393224 | tf_op jit(solution)/shard_map/ppermute | solution.py:221
  84.7 46.3 %collective-permute-start.7 = (bf16[1,32,16,128]{3,2,1,0:T(8,128)(2,1)S(1)}, bf16[1,32,16,128]{3,2,1,0:T(8,128)(2,1)S(1)}, u32[]{:S(2)}, u32[]{:S(2)}) collective-permute-start(bf16[1,32,16,128]{3,2,1,0:T(8,128)(2,1)S(1)} %multiply_convert_fusion.2), channel_id=1, source_target_pairs={{16,0},{17,1},{18,2},{19,3},{20,4},{21,5},{22,6},{23,7},{24,8},{25... | collective-permute-start | bytes 393224 | tf_op jit(solution)/shard_map/ppermute | solution.py:223
  86.2 1.5 %copy-start.26 = (bf16[512,384]{0,1:T(8,128)(2,1)S(1)}, bf16[512,384]{0,1:T(8,128)(2,1)}, u32[]{:S(2)}) copy-start(bf16[512,384]{0,1:T(8,128)(2,1)} %copy.42) | copy-start | bytes 1179652
  86.5 1.5 %copy-start.25 = (bf16[512,384]{0,1:T(8,128)(2,1)S(1)}, bf16[512,384]{0,1:T(8,128)(2,1)}, u32[]{:S(2)}) copy-start(bf16[512,384]{0,1:T(8,128)(2,1)} %copy.43) | copy-start | bytes 1179652
  86.8 1.5 %copy-start.28 = (bf16[512,384]{0,1:T(8,128)(2,1)S(1)}, bf16[512,384]{0,1:T(8,128)(2,1)}, u32[]{:S(2)}) copy-start(bf16[512,384]{0,1:T(8,128)(2,1)} %copy.44) | copy-start | bytes 1179652
  87.1 1.5 %copy-start.27 = (bf16[512,384]{0,1:T(8,128)(2,1)S(1)}, bf16[512,384]{0,1:T(8,128)(2,1)}, u32[]{:S(2)}) copy-start(bf16[512,384]{0,1:T(8,128)(2,1)} %copy.45) | copy-start | bytes 1179652
  88.9 1.5 %copy-start.9 = (bf16[512,384]{0,1:T(8,128)(2,1)S(1)}, bf16[512,384]{0,1:T(8,128)(2,1)}, u32[]{:S(2)}) copy-start(bf16[512,384]{0,1:T(8,128)(2,1)} %copy.28) | copy-start | bytes 1179652
  88.9 1.8 %copy-start.10 = (bf16[512,384]{0,1:T(8,128)(2,1)S(1)}, bf16[512,384]{0,1:T(8,128)(2,1)}, u32[]{:S(2)}) copy-start(bf16[512,384]{0,1:T(8,128)(2,1)} %copy.29) | copy-start | bytes 1179652
  90.4 1.2 copy-start.13
  90.5 1.5 copy-start.12
  90.5 1.8 %copy-start.15 = (bf16[512,384]{0,1:T(8,128)(2,1)S(1)}, bf16[512,384]{0,1:T(8,128)(2,1)}, u32[]{:S(2)}) copy-start(bf16[512,384]{0,1:T(8,128)(2,1)} %copy.33) | copy-start | bytes 1179652
  90.5 2.1 %copy-start.14 = (bf16[512,384]{0,1:T(8,128)(2,1)S(1)}, bf16[512,384]{0,1:T(8,128)(2,1)}, u32[]{:S(2)}) copy-start(bf16[512,384]{0,1:T(8,128)(2,1)} %copy.34) | copy-start | bytes 1179652
  90.8 2.1 %copy-start.17 = (bf16[512,384]{0,1:T(8,128)(2,1)S(1)}, bf16[512,384]{0,1:T(8,128)(2,1)}, u32[]{:S(2)}) copy-start(bf16[512,384]{0,1:T(8,128)(2,1)} %copy.35) | copy-start | bytes 1179652
  91.3 1.8 %copy-start.16 = (bf16[512,384]{0,1:T(8,128)(2,1)S(1)}, bf16[512,384]{0,1:T(8,128)(2,1)}, u32[]{:S(2)}) copy-start(bf16[512,384]{0,1:T(8,128)(2,1)} %copy.36) | copy-start | bytes 1179652
  131.0 3.8 %collective-permute-start.8 = (bf16[3,1,16,128]{3,2,1,0:T(8,128)(2,1)S(1)}, bf16[3,1,16,128]{3,2,1,0:T(8,128)(2,1)S(1)}, u32[]{:S(2)}, u32[]{:S(2)}) collective-permute-start(bf16[3,1,16,128]{3,2,1,0:T(8,128)(2,1)S(1)} %get-tuple-element.121), channel_id=1, source_target_pairs={{0,4},{4,8},{8,12},{1,5},{5,9},{9,13},{2,6},{6,10},{10,14},{3,7},{... | collective-permute-start | bytes 36872 | tf_op jit(solution)/shard_map/ppermute | solution.py:221
  133.3 3.7 %collective-permute-start.9 = (bf16[3,1,16,128]{3,2,1,0:T(8,128)(2,1)S(1)}, bf16[3,1,16,128]{3,2,1,0:T(8,128)(2,1)S(1)}, u32[]{:S(2)}, u32[]{:S(2)}) collective-permute-start(bf16[3,1,16,128]{3,2,1,0:T(8,128)(2,1)S(1)} %get-tuple-element.120), channel_id=1, source_target_pairs={{4,0},{8,4},{12,8},{5,1},{9,5},{13,9},{6,2},{10,6},{14,10},{7,3},{... | collective-permute-start | bytes 36872 | tf_op jit(solution)/shard_map/ppermute | solution.py:223
  137.1 6.1 %collective-permute-start.10 = (bf16[3,34,1,128]{3,2,1,0:T(2,128)(2,1)S(1)}, bf16[3,34,1,128]{3,2,1,0:T(2,128)(2,1)S(1)}, u32[]{:S(2)}, u32[]{:S(2)}) collective-permute-start(bf16[3,34,1,128]{3,2,1,0:T(2,128)(2,1)S(1)} %get-tuple-element.112), channel_id=1, source_target_pairs={{0,1},{1,2},{2,3},{4,5},{5,6},{6,7},{8,9},{9,10},{10,11},{12,13},{... | collective-permute-start | bytes 78344 | tf_op jit(solution)/shard_map/ppermute | solution.py:221
  139.9 6.0 %collective-permute-start.11 = (bf16[3,34,1,128]{3,2,1,0:T(2,128)(2,1)S(1)}, bf16[3,34,1,128]{3,2,1,0:T(2,128)(2,1)S(1)}, u32[]{:S(2)}, u32[]{:S(2)}) collective-permute-start(bf16[3,34,1,128]{3,2,1,0:T(2,128)(2,1)S(1)} %get-tuple-element.113), channel_id=1, source_target_pairs={{1,0},{2,1},{3,2},{5,4},{6,5},{7,6},{9,8},{10,9},{11,10},{13,12},{... | collective-permute-start | bytes 78344 | tf_op jit(solution)/shard_map/ppermute | solution.py:223
  146.7 1.2 copy-start.38
  148.2 1.2 copy-start.52
  148.4 1.3 copy-start.35
  (18 other events, 17.6 us)

commit v2 on v1

--- a/solution.py
+++ b/solution.py
@@ -176,135 +176,323 @@
     return found
 
 
-def reduce_kernel(sizes, ranges, part_ref, out_ref, *scratch):
+DIRS = [(dt, dh) for dt in (-1, 0, 1) for dh in (-1, 0, 1) if (dt, dh) != (0, 0)]
+
+
+class Halo:
+    def __init__(self, sizes, where, sources, landings, send, recv):
+        self.s, self.where = sizes, where
+        self.sources, self.landings = sources, landings
+        self.frames, self.height = sources[0].shape[0], sources[0].shape[1]
+        self.send, self.recv = send, recv
+
+    def exists(self, dt, dh):
+        ti, hi = self.where[0] + dt, self.where[1] + dh
+        return (ti >= 0) & (ti < self.s.nt) & (hi >= 0) & (hi < self.s.nh)
+
+    def made(self, field, dt, dh):
+        def span(step, extent):
+            first = {-1: 0, 0: 0, 1: extent - 1}[step]
+            land = {-1: extent + 1, 0: 1, 1: 0}[step]
+            return first, land, extent if step == 0 else 1
+
+        t0, t1, tn = span(dt, self.frames)
+        h0, h1, hn = span(dh, self.height)
+        slot = field * len(DIRS) + DIRS.index((dt, dh))
+        return pltpu.make_async_remote_copy(
+            src_ref=self.sources[field].at[pl.ds(t0, tn), pl.ds(h0, hn)],
+            dst_ref=self.landings[field].at[pl.ds(t1, tn), pl.ds(h1, hn)],
+            send_sem=self.send.at[slot],
+            recv_sem=self.recv.at[slot],
+            device_id=(self.where[0] + dt, self.where[1] + dh, self.where[2]),
+            device_id_type=MESH,
+        )
+
+    def start(self):
+        for dt, dh in DIRS:
+
+            @pl.when(self.exists(dt, dh))
+            def _():
+                for field in range(len(self.sources)):
+                    self.made(field, dt, dh).start()
+
+    def zero(self):
+        def span(step, extent):
+            return {-1: (0, 1), 0: (1, extent), 1: (extent + 1, 1)}[step]
+
+        for dt, dh in DIRS:
+
+            @pl.when(jnp.logical_not(self.exists(dt, dh)))
+            def _():
+                for landing in self.landings:
+                    part = landing.at[pl.ds(*span(dt, self.frames)), pl.ds(*span(dh, self.height))]
+                    part[...] = jnp.zeros(part.shape, part.dtype)
+
+    def wait_recv(self):
+        for dt, dh in DIRS:
+
+            @pl.when(self.exists(-dt, -dh))
+            def _():
+                for field in range(len(self.sources)):
+                    self.made(field, dt, dh).wait_recv()
+
+    def wait_send(self):
+        for dt, dh in DIRS:
+
+            @pl.when(self.exists(dt, dh))
+            def _():
+                for field in range(len(self.sources)):
+                    self.made(field, dt, dh).wait_send()
+
+
+class Columns:
+    def __init__(self, sizes, where, landings, lines, shifted, edge_out, edge_in, wide, send, recv):
+        self.s, self.where, self.landings, self.lines = sizes, where, landings, lines
+        self.shifted, self.out, self.into, self.wide = shifted, edge_out, edge_in, wide
+        self.send, self.recv = send, recv
+        self.count = landings[0].shape[0] * landings[0].shape[1]
+        self.width = landings[0].shape[2]
+
+    def exists(self, side):
+        to = self.where[2] + (1 if side else -1)
+        return (to >= 0) & (to < self.s.nw)
+
+    def made(self, side):
+        return pltpu.make_async_remote_copy(
+            src_ref=self.out.at[side],
+            dst_ref=self.into.at[1 - side],
+            send_sem=self.send.at[side],
+            recv_sem=self.recv.at[1 - side],
+            device_id=(self.where[0], self.where[1], self.where[2] + (1 if side else -1)),
+            device_id_type=MESH,
+        )
+
+    def start(self):
+        cells = self.count * self.width
+        for field, landing in enumerate(self.landings):
+            line = self.lines[field]
+            line[pl.ds(8, cells), :] = landing[...].astype(jnp.float32).reshape(cells, 128)
+            for side in range(2):
+                edge = line[pl.ds(8 + side * (self.width - 1), self.count, stride=self.width), :]
+                self.out[side, field] = edge.astype(jnp.bfloat16)
+        for side in range(2):
+            pl.when(self.exists(side))(lambda side=side: self.made(side).start())
+            zero = jnp.zeros(self.into.shape[1:], jnp.bfloat16)
+
+            @pl.when(jnp.logical_not(self.exists(side)))
+            def _():
+                self.into[side] = zero
+
+        frames = self.landings[0].shape[0]
+        for field, landing in enumerate(self.landings):
+            self.wide[field, :, :, 128:256] = landing[...].reshape(frames, -1, 128)
+
+    def finish(self):
+        for side in range(2):
+            pl.when(self.exists(side))(lambda side=side: self.made(1 - side).wait_recv())
+        cells = self.count * self.width
+        frames = self.landings[0].shape[0]
+        for field in range(len(self.landings)):
+            for side in range(2):
+                line = self.lines[field]
+                self.shifted[...] = line[pl.ds(7 + 2 * side, cells), :]
+                at = side * (self.width - 1)
+                edge = self.into[side, field].astype(jnp.float32)
+                self.shifted[pl.ds(at, self.count, stride=self.width), :] = edge
+                moved = self.shifted[...].astype(jnp.bfloat16).reshape(frames, -1, 128)
+                self.wide[field, :, :, 256 * side : 256 * side + 128] = moved
+
+    def wait_send(self):
+        for side in range(2):
+            pl.when(self.exists(side))(lambda side=side: self.made(side).wait_send())
+
+
+def conv_rows(wide, field, frame, first, rows, width, weights):
+    total = None
+    for tap in range(9):
+        at = (tap % 3) * width + first
+        piece = wide[field, frame + tap // 3, pl.ds(at, rows), :]
+        product = jnp.dot(piece, weights[tap], preferred_element_type=jnp.float32)
+        total = product if total is None else total + product
+    return total
+
+
+def kernel(
+    sizes, ranges, volume, cotangent, one, two, d_volume, sums,
+    fields, d_fields, lines, shifted, edge_out, edge_in, d_out, d_in, wide, d_wide,
+    flip_one, flip_two, d_pre, part, turned, halo_send, halo_recv, col_send, col_recv, *scratch,
+):
     bufs, (send, recv) = scratch[:4], scratch[4:]
     where = (lax.axis_index("ta"), lax.axis_index("ha"), lax.axis_index("wa"))
+    frames, height, width, _ = volume.shape
+    cells = height * width
+    block = 256 if cells % 256 == 0 else cells
     partners = reduce_partners(sizes, where)
+    halo = Halo(
+        sizes, where, [volume, cotangent], [fields.at[0], fields.at[1]], halo_send.at[0], halo_recv.at[0]
+    )
+    d_halo = Halo(sizes, where, [d_pre], [d_fields], halo_send.at[1], halo_recv.at[1])
     barrier = pltpu.get_barrier_semaphore()
     for device in partners:
         pl.semaphore_signal(barrier, inc=1, device_id=device, device_id_type=MESH)
-    pl.semaphore_wait(barrier, len(partners))
+    for dt, dh in DIRS:
+
+        @pl.when(halo.exists(dt, dh))
+        def _():
+            device = (where[0] + dt, where[1] + dh, where[2])
+            pl.semaphore_signal(barrier, inc=1, device_id=device, device_id_type=MESH)
+
+    near = sum(halo.exists(dt, dh).astype(jnp.int32) for dt, dh in DIRS)
+    pl.semaphore_wait(barrier, len(partners) + near)
+    halo.start()
+    halo.zero()
+    d_halo.zero()
+    inner = (pl.ds(1, frames), pl.ds(1, height))
+    for field, ref in enumerate((volume, cotangent)):
+        fields.at[field].at[inner][...] = ref[...]
+    for source, flipped in ((two, flip_two), (one, flip_one)):
+        for tap in range(9):
+            for kw in range(3):
+                square = source[8 - tap, pl.ds((2 - kw) * 128, 128), :].astype(jnp.float32)
+                flipped[tap, pl.ds(kw * 128, 128), :] = square.T.astype(jnp.bfloat16)
+    halo.wait_recv()
+    columns = Columns(
+        sizes, where, [fields.at[0], fields.at[1]], [lines.at[0], lines.at[1]], shifted,
+        edge_out, edge_in, wide, col_send.at[0], col_recv.at[0],
+    )
+    columns.start()
+    columns.finish()
+    for frame in range(frames):
+        for first in range(0, cells, block):
+            pre = conv_rows(wide, 0, frame, first, block, width, one)
+            d_hidden = conv_rows(wide, 1, frame, first, block, width, flip_two)
+            sig = 1.0 / (1.0 + jnp.exp(-pre))
+            hidden = pre * sig
+            grad = d_hidden * sig * (1.0 + pre * (1.0 - sig))
+            at = pl.ds(frame * cells + first, block)
+            turned[0, :, at] = hidden.T.astype(jnp.bfloat16)
+            turned[1, :, at] = grad.T.astype(jnp.bfloat16)
+            rounded = grad.astype(jnp.bfloat16).reshape(1, block // width, width, 128)
+            d_pre[pl.ds(frame, 1), pl.ds(first // width, block // width)] = rounded
+    d_halo.start()
+    d_fields.at[inner][...] = d_pre[...]
+    middle = part.shape[0] // 2
+    real = 27 * 128 // TILE
+    for base in (0, middle):
+        if middle > real:
+            part[pl.ds(base + real, middle - real)] = jnp.zeros((middle - real, TILE, 128), jnp.bfloat16)
+
+    def gradient(field, side, tap):
+        total = None
+        for frame in range(frames):
+            piece = wide[field, frame + tap // 3, pl.ds((tap % 3) * width, cells), :]
+            left = turned[side, :, pl.ds(frame * cells, cells)]
+            product = jnp.dot(left, piece, preferred_element_type=jnp.float32)
+            total = product if total is None else total + product
+        return total
+
+    for tap in range(9):
+        product = gradient(1, 0, tap).astype(jnp.bfloat16)
+        for kw in range(3):
+            at = ((8 - tap) * 3 + 2 - kw) * (128 // TILE)
+            square = product[:, kw * 128 : kw * 128 + 128]
+            part[pl.ds(at, 128 // TILE)] = square.reshape(128 // TILE, TILE, 128)
     runs = [
-        Reduce(sizes, where, part_ref, out_ref, first, tiles, first, bufs, send, recv, i * copies_of(sizes))
+        Reduce(sizes, where, part, sums, first, tiles, first, bufs, send, recv, i * copies_of(sizes))
         for i, (first, tiles) in enumerate(ranges)
     ]
-    for stage in STAGES:
+    early, late = runs[: len(runs) // 2], runs[len(runs) // 2 :]
+    for run in early:
+        run.start_core()
+    for tap in range(9):
+        product = gradient(0, 1, tap)
+        for kw in range(3):
+            at = middle + (tap * 3 + kw) * (128 // TILE)
+            square = product[:, kw * 128 : kw * 128 + 128].T.astype(jnp.bfloat16)
+            part[pl.ds(at, 128 // TILE)] = square.reshape(128 // TILE, TILE, 128)
+    for run in late:
+        run.start_core()
+    for run in early:
+        run.start_plane()
+    d_halo.wait_recv()
+    d_columns = Columns(
+        sizes, where, [d_fields], [lines.at[0]], shifted, d_out, d_in, d_wide, col_send.at[1], col_recv.at[1]
+    )
+    d_columns.start()
+    for run in late:
+        run.start_plane()
+    d_columns.finish()
+    for frame in range(frames):
+        for first in range(0, cells, block):
+            total = conv_rows(d_wide, 0, frame, first, block, width, flip_one)
+            total = total.astype(jnp.bfloat16).reshape(1, block // width, width, 128)
+            d_volume[pl.ds(frame, 1), pl.ds(first // width, block // width)] = total
+    for stage in STAGES[2:]:
         for run in runs:
             getattr(run, stage)()
-
-
-def all_sum(sizes, parts, pieces):
-    total = parts.shape[0]
-    ranges = chunks_of(total, sizes.devices, pieces)
-    tiles = sum(size for _, size in ranges)
-    parts = jnp.pad(parts, ((0, tiles - total), (0, 0), (0, 0)))
-    return pl.pallas_call(
-        functools.partial(reduce_kernel, sizes, ranges),
-        out_shape=jax.ShapeDtypeStruct((tiles, TILE, 128), jnp.bfloat16),
-        in_specs=[pl.BlockSpec(memory_space=pltpu.VMEM)],
-        out_specs=pl.BlockSpec(memory_space=pltpu.VMEM),
-        scratch_shapes=reduce_scratch(sizes, tiles, len(ranges)),
+    halo.wait_send()
+    d_halo.wait_send()
+    columns.wait_send()
+    d_columns.wait_send()
+
+
+def body(sizes, volume, cotangent, kernel_one, kernel_two):
+    frames, height, width, chans = volume.shape
+    real = 27 * chans // TILE
+    ranges = chunks_of(real, sizes.devices, 2)
+    middle = sum(tiles for _, tiles in ranges)
+    ranges = ranges + [(middle + first, tiles) for first, tiles in ranges]
+    tiles = 2 * middle
+    tall, high = frames + 2, height + 2
+    count = tall * high
+    half = jnp.bfloat16
+    vmem = pl.BlockSpec(memory_space=pltpu.VMEM)
+    d_volume, sums = pl.pallas_call(
+        functools.partial(kernel, sizes, ranges),
+        out_shape=(
+            jax.ShapeDtypeStruct(volume.shape, half),
+            jax.ShapeDtypeStruct((tiles, TILE, chans), half),
+        ),
+        in_specs=[vmem] * 4,
+        out_specs=(vmem, vmem),
+        scratch_shapes=[
+            pltpu.VMEM((2, tall, high, width, chans), half),
+            pltpu.VMEM((tall, high, width, chans), half),
+            pltpu.VMEM((2, count * width + 16, chans), jnp.float32),
+            pltpu.VMEM((count * width, chans), jnp.float32),
+            pltpu.VMEM((2, 2, count, chans), half),
+            pltpu.VMEM((2, 2, count, chans), half),
+            pltpu.VMEM((2, 1, count, chans), half),
+            pltpu.VMEM((2, 1, count, chans), half),
+            pltpu.VMEM((2, tall, high * width, 3 * chans), half),
+            pltpu.VMEM((1, tall, high * width, 3 * chans), half),
+            pltpu.VMEM((9, 3 * chans, chans), half),
+            pltpu.VMEM((9, 3 * chans, chans), half),
+            pltpu.VMEM(volume.shape, half),
+            pltpu.VMEM((tiles, TILE, chans), half),
+            pltpu.VMEM((2, chans, frames * height * width), half),
+            pltpu.SemaphoreType.DMA((2, 2 * len(DIRS))),
+            pltpu.SemaphoreType.DMA((2, 2 * len(DIRS))),
+            pltpu.SemaphoreType.DMA((2, 2)),
+            pltpu.SemaphoreType.DMA((2, 2)),
+        ]
+        + reduce_scratch(sizes, tiles, len(ranges)),
         compiler_params=pltpu.CompilerParams(
-            collective_id=0, has_side_effects=True, vmem_limit_bytes=48 * 1024 * 1024
+            collective_id=0, has_side_effects=True, vmem_limit_bytes=56 * 1024 * 1024
         ),
-    )(parts)[:total]
-
-
-def padded_2(cells, sides, width):
-    for axis, dim in sides:
-        count = lax.axis_size(axis)
-        ends = count - 1
-        head = lax.slice_in_dim(cells, 0, width, axis=dim)
-        tail = lax.slice_in_dim(cells, cells.shape[dim] - width, cells.shape[dim], axis=dim)
-        cells = jnp.concatenate(
-            [
-                lax.ppermute(tail, axis, [(i, (i + 1) % count) for i in range(ends)]),
-                cells,
-                lax.ppermute(head, axis, [((i + 1) % count, i) for i in range(ends)]),
-            ],
-            axis=dim,
-        )
-    return cells
-
-
-def flip_swap(kernel):
-    return jnp.swapaxes(kernel[::-1, ::-1, ::-1], 3, 4)
-
-
-def window_rows(padded, offset_t, offset_h):
-    frames = padded.shape[0] - 2
-    height = padded.shape[1] - 2
-    width = padded.shape[2] - 2
-    chans = padded.shape[3]
-    pieces = [
-        padded[offset_t : offset_t + frames, offset_h : offset_h + height, shift : shift + width]
-        for shift in range(3)
-    ]
-    return jnp.concatenate(pieces, axis=-1).reshape(-1, 3 * chans)
-
-
-def conv_local(padded, kernel):
-    frames = padded.shape[0] - 2
-    height = padded.shape[1] - 2
-    width = padded.shape[2] - 2
-    chans = padded.shape[3]
-    total = jnp.zeros((frames * height * width, chans), jnp.float32)
-    for offset_t in range(3):
-        for offset_h in range(3):
-            rows = window_rows(padded, offset_t, offset_h)
-            total = total + jnp.dot(
-                rows,
-                kernel[offset_t, offset_h].reshape(3 * chans, chans),
-                preferred_element_type=jnp.float32,
-            )
-    return total.reshape(frames, height, width, chans)
-
-
-def kernel_local(padded, other):
-    chans = padded.shape[3]
-    right = other.reshape(-1, chans)
-    blocks = []
-    for offset_t in range(3):
-        for offset_h in range(3):
-            rows = window_rows(padded, offset_t, offset_h)
-            product = lax.dot_general(
-                rows, right, (((0,), (0,)), ((), ())), preferred_element_type=jnp.float32
-            )
-            blocks.append(product.reshape(3, chans, chans))
-    return jnp.stack(blocks).reshape(3, 3, 3, chans, chans)
-
-
-def body(sizes, volume, cotangent, kernel_one, kernel_two):
-    stacked = jnp.stack((volume, cotangent))
-    padded_both = padded_2(stacked, (("ta", 1), ("ha", 2), ("wa", 3)), 1)
-    volume_pad = padded_both[0]
-    cotangent_pad = padded_both[1]
-    pre = conv_local(volume_pad, kernel_one)
-    sig = jax.nn.sigmoid(pre)
-    hidden = (pre * sig).astype(jnp.bfloat16)
-    d_hidden = conv_local(cotangent_pad, flip_swap(kernel_two))
-    d_pre = (d_hidden * sig * (1.0 + pre * (1.0 - sig))).astype(jnp.bfloat16)
-    total_cells = (
-        volume.shape[0]
-        * volume.shape[1]
-        * volume.shape[2]
-        * lax.axis_size("ta")
-        * lax.axis_size("ha")
-        * lax.axis_size("wa")
-    )
-    scale = 1.0 / jnp.sqrt(jnp.float32(total_cells))
-    part_two = flip_swap(kernel_local(cotangent_pad, hidden))
-    d_pre_pad = padded_2(d_pre, (("ta", 0), ("ha", 1), ("wa", 2)), 1)
-    d_volume = conv_local(d_pre_pad, flip_swap(kernel_one)).astype(jnp.bfloat16)
-    part_one = kernel_local(volume_pad, d_pre)
-    both = jnp.concatenate([part_one.reshape(-1), part_two.reshape(-1)]).astype(jnp.bfloat16)
-    summed = all_sum(sizes, both.reshape(-1, TILE, 128), 4).reshape((2,) + kernel_one.shape)
-    summed = summed.astype(jnp.float32) * scale
-    return (d_volume, summed[0], summed[1])
+    )(volume, cotangent, kernel_one.reshape(9, 3 * chans, chans), kernel_two.reshape(9, 3 * chans, chans))
+    scale = 1.0 / jnp.sqrt(jnp.float32(frames * height * width * sizes.devices))
+
+    def scaled(first):
+        return sums[first : first + real].reshape(kernel_one.shape).astype(jnp.float32) * scale
+
+    return d_volume, scaled(middle), scaled(0)
 
 
 def solution(mesh):
     in_specs = (P("ta", "ha", "wa", None), P("ta", "ha", "wa", None), P(), P())
     out_specs = (P("ta", "ha", "wa", None), P(), P())
     return jax.shard_map(
-        functools.partial(body, Sizes(mesh)), mesh=mesh, in_specs=in_specs, out_specs=out_specs, check_vma=False)
+        functools.partial(body, Sizes(mesh)),
+        mesh=mesh, in_specs=in_specs, out_specs=out_specs, check_vma=False,
+    )

time: 153 us -> 61.1 us (0.40)
  local copies, waits for them, and re-layouts: 39.5 us -> 0.66 us
  starting transfers between devices: 24.9 us -> 0 us
  Pallas kernels: 37.2 us -> 56.1 us
  matrix products: 18.2 us -> 0 us
  waiting for transfers between devices: 15.1 us -> 0 us
  other arithmetic: 14.9 us -> 3.54 us
    ppermute x12 -> x0, starting transfers between devices: 24.9 us -> none  [the longest x6 17 us: padded_2(): lax.ppermute(tail, axis, [(i, (i + 1) % count) for i in range(ends)])]
    reshape x19 -> x0, local copies, waits for them, and re-layouts: 24.3 us -> none  [the longest x18 22.9 us: window_rows(): return jnp.concatenate(pieces, axis=-1).reshape(-1, 3 * chans)]
    pallas_call x1, Pallas kernels: 37.2 us -> 56.1 us  [body(): pl.pallas_call(functools.partial(kernel, sizes, ranges), out_shape=(jax.S...]
    dot_general x45 -> x0, matrix products: 18.2 us -> none  [the longest x27 13 us: conv_local(): jnp.dot(rows, kernel[offset_t, offset_h].reshape(3 * chans, chans), prefe...]
    ppermute x12 -> x0, waiting for transfers between devices: 15.1 us -> none  [the longest x6 15.1 us: padded_2(): lax.ppermute(head, axis, [((i + 1) % count, i) for i in range(ends)])]
    concatenate x20 -> x0, other arithmetic: 12.5 us -> none  [the longest x16 10.9 us: window_rows(): return jnp.concatenate(pieces, axis=-1).reshape(-1, 3 * chans)]
    slice x9 -> x0, local copies, waits for them, and re-layouts: 9.95 us -> none  [the longest x3 4.12 us: conv_local(): kernel[offset_t, offset_h].reshape(3 * chans, chans)]
    unnamed x110 -> x3, local copies, waits for them, and re-layouts: 4.81 us -> 0.66 us
  transfers between devices with their start and end apart: 12 -> 0, of which waited for: 5 -> 0; matrix products, arithmetic and copies ran while one was open for 11% -> 0% of each run, Pallas kernels for 25% -> 0%
where the time goes in v2:
time: 61.1 us; the launch traced here: 60.9 us
  Pallas kernels  56.1 us (92%)
  other arithmetic  3.54 us (6%)
  local copies, waits for them, and re-layouts  0.66 us (1%)
  between operations  0.65 us (1%)
    pallas_call x1, Pallas kernels, body(): pl.pallas_call(functools.partial(kernel, sizes, ranges), out_shape=(jax.S...  56.1 us
    mul x1, other arithmetic, scaled(): sums[first:first + real].reshape(kernel_one.shape).astype(jnp.float32)  3.54 us

profile of v2, /device:TPU:0, one launch (start us, length us, event | category | flops | bytes accessed | tf_op | source)
XLA Modules:
  0.0 60.9 jit_solution(11355710374790020322)
XLA Ops:
  0.6 56.1 %shard_map.67 = (bf16[1,32,16,128]{3,2,1,0:T(8,128)(2,1)}, bf16[448,16,128]{2,1,0:T(8,128)(2,1)}) custom-call(bf16[1,32,16,128]{3,2,1,0:T(8,128)(2,1)} %volume.1, bf16[1,32,16,128]{3,2,1,0:T(8,128)(2,1)} %cotangent.1, bf16[9,384,128]{2,1,0:T(8,128)(2,1)} %bitcast.6, bf16[9,384,128]{2,1,0:T(8,128)(2,1)} %bitcast.7), custom_call_target="tpu_custom_call" | custom-call | tf_op jit(solution)/shard_map/pallas_call | solution.py:450
  56.7 0.0 copy-start
  56.7 3.5 %convert_multiply_fusion = (f32[216,16,128]{2,1,0:T(8,128)}, f32[216,16,128]{2,1,0:T(8,128)}) fusion(bf16[448,16,128]{2,1,0:T(8,128)(2,1)} %get-tuple-element.6), kind=kLoop, calls=%fused_computation | loop fusion | flops 1769472 | bytes 5308416 | tf_op jit(solution)/shard_map/mul | solution.py:487
  60.2 0.0 copy-done
  60.2 0.7 %copy.8 = bf16[1,32,16,128]{3,2,1,0:T(8,128)(2,1)} copy(bf16[1,32,16,128]{3,2,1,0:T(8,128)(2,1)S(1)} %copy-done) | data formatting | bytes 262144
Async XLA Ops:
  56.7 3.6 %copy-start = (bf16[1,32,16,128]{3,2,1,0:T(8,128)(2,1)S(1)}, bf16[1,32,16,128]{3,2,1,0:T(8,128)(2,1)}, u32[]{:S(2)}) copy-start(bf16[1,32,16,128]{3,2,1,0:T(8,128)(2,1)} %get-tuple-element.12) | copy-start | bytes 393220

commit v3 on v2

--- a/solution.py
+++ b/solution.py
@@ -32,6 +32,7 @@
         self.s, self.source, self.out = sizes, source, out
         self.ti, self.hi, self.wi = where
         self.core = self.hi % sizes.cores
+        self.tiles = tiles
         self.half = tiles // sizes.cores
         self.part = self.half // sizes.plane
         self.shard = self.part // sizes.nw
@@ -391,28 +392,36 @@
             total = product if total is None else total + product
         return total
 
-    for tap in range(9):
-        product = gradient(1, 0, tap).astype(jnp.bfloat16)
-        for kw in range(3):
-            at = ((8 - tap) * 3 + 2 - kw) * (128 // TILE)
-            square = product[:, kw * 128 : kw * 128 + 128]
-            part[pl.ds(at, 128 // TILE)] = square.reshape(128 // TILE, TILE, 128)
     runs = [
         Reduce(sizes, where, part, sums, first, tiles, first, bufs, send, recv, i * copies_of(sizes))
         for i, (first, tiles) in enumerate(ranges)
     ]
     early, late = runs[: len(runs) // 2], runs[len(runs) // 2 :]
-    for run in early:
-        run.start_core()
+
+    def begin(group, base, tap):
+        done = middle if tap == 8 else (tap + 1) * 3 * (128 // TILE)
+        while group and group[0].first + group[0].tiles - base <= done:
+            group.pop(0).start_core()
+
+    waiting = list(early)
+    for tap in range(9):
+        product = gradient(1, 0, 8 - tap).astype(jnp.bfloat16)
+        for kw in range(3):
+            at = (tap * 3 + 2 - kw) * (128 // TILE)
+            square = product[:, kw * 128 : kw * 128 + 128]
+            part[pl.ds(at, 128 // TILE)] = square.reshape(128 // TILE, TILE, 128)
+        begin(waiting, 0, tap)
+    waiting, plane = list(late), list(early)
     for tap in range(9):
         product = gradient(0, 1, tap)
         for kw in range(3):
             at = middle + (tap * 3 + kw) * (128 // TILE)
             square = product[:, kw * 128 : kw * 128 + 128].T.astype(jnp.bfloat16)
             part[pl.ds(at, 128 // TILE)] = square.reshape(128 // TILE, TILE, 128)
-    for run in late:
-        run.start_core()
-    for run in early:
+        begin(waiting, middle, tap)
+        if tap % 3 == 1 and plane:
+            plane.pop(0).start_plane()
+    for run in plane:
         run.start_plane()
     d_halo.wait_recv()
     d_columns = Columns(
@@ -421,15 +430,24 @@
     d_columns.start()
     for run in late:
         run.start_plane()
-    d_columns.finish()
-    for frame in range(frames):
-        for first in range(0, cells, block):
-            total = conv_rows(d_wide, 0, frame, first, block, width, flip_one)
-            total = total.astype(jnp.bfloat16).reshape(1, block // width, width, 128)
-            d_volume[pl.ds(frame, 1), pl.ds(first // width, block // width)] = total
-    for stage in STAGES[2:]:
-        for run in runs:
-            getattr(run, stage)()
+
+    def volume_part():
+        d_columns.finish()
+        for frame in range(frames):
+            for first in range(0, cells, block):
+                total = conv_rows(d_wide, 0, frame, first, block, width, flip_one)
+                total = total.astype(jnp.bfloat16).reshape(1, block // width, width, 128)
+                d_volume[pl.ds(frame, 1), pl.ds(first // width, block // width)] = total
+
+    order = STAGES[2:-1]
+    for wave in range(len(runs) + len(order) - 1):
+        for place, run in enumerate(runs):
+            if 0 <= wave - place < len(order):
+                getattr(run, order[wave - place])()
+        if wave == 0:
+            volume_part()
+    for run in runs:
+        run.finish()
     halo.wait_send()
     d_halo.wait_send()
     columns.wait_send()
@@ -439,7 +457,7 @@
 def body(sizes, volume, cotangent, kernel_one, kernel_two):
     frames, height, width, chans = volume.shape
     real = 27 * chans // TILE
-    ranges = chunks_of(real, sizes.devices, 2)
+    ranges = chunks_of(real, sizes.devices, 3)
     middle = sum(tiles for _, tiles in ranges)
     ranges = ranges + [(middle + first, tiles) for first, tiles in ranges]
     tiles = 2 * middle

time: 61.1 us -> 67.1 us (1.098)
  Pallas kernels: 56.1 us -> 62.1 us
    pallas_call x1, Pallas kernels: 56.1 us -> 62.1 us  [body(): pl.pallas_call(functools.partial(kernel, sizes, ranges), out_shape=(jax.S...]
where the time goes in v3:
time: 67.1 us; the launch traced here: 66.9 us
  Pallas kernels  62.1 us (93%)
  other arithmetic  3.54 us (5%)
    pallas_call x1, Pallas kernels, body(): pl.pallas_call(functools.partial(kernel, sizes, ranges), out_shape=(jax.S...  62.1 us
    mul x1, other arithmetic, scaled(): sums[first:first + real].reshape(kernel_one.shape).astype(jnp.float32)  3.54 us

profile of v3, /device:TPU:0, one launch (start us, length us, event | category | flops | bytes accessed | tf_op | source)
XLA Modules:
  0.0 66.9 jit_solution(4576619487832944985)
XLA Ops:
  0.6 62.1 %shard_map.67 = (bf16[1,32,16,128]{3,2,1,0:T(8,128)(2,1)}, bf16[448,16,128]{2,1,0:T(8,128)(2,1)}) custom-call(bf16[1,32,16,128]{3,2,1,0:T(8,128)(2,1)} %volume.1, bf16[1,32,16,128]{3,2,1,0:T(8,128)(2,1)} %cotangent.1, bf16[9,384,128]{2,1,0:T(8,128)(2,1)} %bitcast.6, bf16[9,384,128]{2,1,0:T(8,128)(2,1)} %bitcast.7), custom_call_target="tpu_custom_call" | custom-call | tf_op jit(solution)/shard_map/pallas_call | solution.py:468
  62.7 0.0 copy-start
  62.7 3.5 %convert_multiply_fusion = (f32[216,16,128]{2,1,0:T(8,128)}, f32[216,16,128]{2,1,0:T(8,128)}) fusion(bf16[448,16,128]{2,1,0:T(8,128)(2,1)} %get-tuple-element.6), kind=kLoop, calls=%fused_computation | loop fusion | flops 1769472 | bytes 5308416 | tf_op jit(solution)/shard_map/mul | solution.py:505
  66.3 0.0 copy-done
  66.3 0.7 copy.8
Async XLA Ops:
  62.7 3.6 %copy-start = (bf16[1,32,16,128]{3,2,1,0:T(8,128)(2,1)S(1)}, bf16[1,32,16,128]{3,2,1,0:T(8,128)(2,1)}, u32[]{:S(2)}) copy-start(bf16[1,32,16,128]{3,2,1,0:T(8,128)(2,1)} %get-tuple-element.12) | copy-start | bytes 393220
